TPU v7x, 128 devices: a whole 4x4x4 slice. The times are simulated.
128 devices in a mesh: fsdp: 16 (over z, x), model: 8 (over y, core).
Axes of the slice: x: 4, y: 4, z: 4, core: 2. Of those that a mesh axis runs over, the one named last changes fastest.
Arguments:
- weight_query: bfloat16 [5120, 8192], P('fsdp', 'model'), may hold values from -0.125 to 0.125
- low_query: bfloat16 [5120, 32], P('fsdp'), may hold values from -0.078125 to 0.078125
- high_query: bfloat16 [32, 8192], P(None, 'model'), may hold values from -1 to 1
- weight_key: bfloat16 [5120, 1024], P('fsdp', 'model'), may hold values from -0.125 to 0.125
- low_key: bfloat16 [5120, 32], P('fsdp'), may hold values from -0.078125 to 0.078125
- high_key: bfloat16 [32, 1024], P(None, 'model'), may hold values from -1 to 1
- weight_value: bfloat16 [5120, 1024], P('fsdp', 'model'), may hold values from -0.125 to 0.125
- low_value: bfloat16 [5120, 32], P('fsdp'), may hold values from -0.078125 to 0.078125
- high_value: bfloat16 [32, 1024], P(None, 'model'), may hold values from -1 to 1
- norm_train: float32 [5120], P(('fsdp', 'model')), may hold values from 0.25 to 1.75
- norm_step: float32 [5120], P(('fsdp', 'model')), may hold values from -0.3 to 0.3
Outputs:
- final_query: bfloat16 [5120, 8192], P(None, 'model')
- final_key: bfloat16 [5120, 1024], P(None, 'model')
- final_value: bfloat16 [5120, 1024], P(None, 'model')
- column_query: float32 [8192], P('model')
- column_key: float32 [1024], P('model')
- column_value: float32 [1024], P('model')
- serve_norm: bfloat16 [5120], replicated
All inputs are finite; a program needn't handle non-finite values. Where the computation divides by a largest or mean magnitude, that divisor is 1e-20 or more.
Results may differ from a plain program's by a relative error of at most 0.001.
Values may be sent and summed in bfloat16 or wider, within the bound.
No kernel may reach another device: no remote copies, remote signals or barrier semaphores. Data moves between devices by JAX's collectives and lax.ppermute only.
A program may use at most 128 MiB of HBM per device.

v0:
```python
import jax
import jax.numpy as jnp
from jax import lax
from jax.sharding import PartitionSpec as P

mix_rate = 0.5


def copy_for_each(shard, axis):
    copies = jnp.broadcast_to(shard, (lax.axis_size(axis), *shard.shape))
    return lax.all_to_all(copies, axis, split_axis=0, concat_axis=0, tiled=True)


def taken_together(shard, axis):
    everything = copy_for_each(shard, axis)
    return jnp.max(everything, axis=0)


def packed_total(arrays, axis):
    ravelled, at, gathered = (jnp.concatenate([a.reshape(-1) for a in arrays]), 0, [])
    running = taken_together(ravelled, axis)
    for a in arrays:
        gathered.append(running[at : at + a.size].reshape(a.shape))
        at += a.size
    return tuple(gathered)


def sent_together(arrays, axis, dim, along):
    widths = [a.shape[along] for a in arrays]
    both = jnp.concatenate(arrays, axis=along)
    out = lax.all_gather(both, axis, axis=dim, tiled=True)
    return tuple(jnp.split(out, [sum(widths[:k]) for k in range(1, len(widths))], axis=along))


def per_device(
    weight_query,
    low_query,
    high_query,
    weight_key,
    low_key,
    high_key,
    weight_value,
    low_value,
    high_value,
    norm_train,
    norm_step,
):
    result_query = weight_query.astype(jnp.float32) + mix_rate * jnp.dot(
        low_query, high_query, preferred_element_type=jnp.float32
    )
    result_key = weight_key.astype(jnp.float32) + mix_rate * jnp.dot(
        low_key, high_key, preferred_element_type=jnp.float32
    )
    result_value = weight_value.astype(jnp.float32) + mix_rate * jnp.dot(
        low_value, high_value, preferred_element_type=jnp.float32
    )
    column_query, column_key, column_value = packed_total(
        (
            jnp.max(jnp.abs(result_query), axis=0),
            jnp.max(jnp.abs(result_key), axis=0),
            jnp.max(jnp.abs(result_value), axis=0),
        ),
        "fsdp",
    )
    narrow_query, narrow_key, narrow_value = (
        (result_query / column_query).astype(jnp.bfloat16),
        (result_key / column_key).astype(jnp.bfloat16),
        (result_value / column_value).astype(jnp.bfloat16),
    )
    final_query, final_key, final_value = sent_together(
        (narrow_query, narrow_key, narrow_value), "fsdp", 0, 1
    )
    serve_norm = lax.all_gather(
        (norm_train + norm_step).astype(jnp.bfloat16), ("fsdp", "model"), axis=0, tiled=True
    )
    return (final_query, final_key, final_value, column_query, column_key, column_value, serve_norm)


def solution(mesh):
    return jax.shard_map(
        per_device,
        mesh=mesh,
        in_specs=(
            P("fsdp", "model"),
            P("fsdp", None),
            P(None, "model"),
            P("fsdp", "model"),
            P("fsdp", None),
            P(None, "model"),
            P("fsdp", "model"),
            P("fsdp", None),
            P(None, "model"),
            P(("fsdp", "model")),
            P(("fsdp", "model")),
        ),
        out_specs=(
            P(None, "model"),
            P(None, "model"),
            P(None, "model"),
            P("model"),
            P("model"),
            P("model"),
            P(),
        ),
        check_vma=False,
    )
```

profile of v0, /device:TPU:1, one launch (start us, length us, event | category | flops | bytes accessed | tf_op | source)
XLA Modules:
  0.0 138.7 jit_solution(13755721544940811369)
XLA Ops:
  7.2 0.0 copy-start
  7.2 0.0 all-gather.2.cloned.1.call-start
  7.3 0.7 copy-done
  8.0 1.5 %abs_reduce_fusion = (f32[1024]{0:T(1024)S(1)}, f32[320,1024]{1,0:T(8,128)S(1)}) fusion(bf16[320,32]{0,1:T(8,128)(2,1)} %param.12, bf16[32,1024]{1,0:T(8,128)(2,1)S(1)} %copy-done, bf16[320,1024]{1,0:T(8,128)(2,1)} %param.11), kind=kOutput, calls=%fused_computation.3 | convolution fusion | flops 22608896 | bytes 2056192 | tf_op jit(solution)/shard_map/dot_general | solution.py:48
  9.5 0.2 abs_reduce_fusion.1
  9.7 0.0 copy-done.2
  9.7 0.0 copy-done.4
  9.8 0.0 copy-done.7
  9.8 0.2 abs_reduce_fusion.2
  10.1 14.8 %all_to_all.6 = f32[16,1,1280]{2,1,0:T(1,128)S(1)} all-to-all(f32[16,1,1280]{2,1,0:T(1,128)S(1)} %broadcast_in_dim.2), channel_id=1, replica_groups=mesh['fsdp'=16,'model'=8] {'fsdp'}, dimensions={0} | all-to-all | bytes 163840 | tf_op jit(solution)/shard_map/all_to_all | solution.py:11
  24.9 0.1 reduce_max.39
  24.9 0.0 copy-start.8
  25.0 0.0 copy-start.9
  25.0 0.0 copy-start.5
  25.0 0.1 divide_convert_fusion
  25.2 0.0 copy-start.10
  25.2 0.0 copy-start.11
  25.2 1.0 pad_maximum_fusion
  26.2 0.0 all-gather.2.cloned.1.call-update
  26.2 0.2 dynamic-update-slice
  26.5 67.2 %all-reduce = bf16[5120]{0:T(1024)(128)(2,1)} all-reduce(bf16[5120]{0:T(1024)(128)(2,1)S(1)} %dynamic-update-slice), channel_id=1, replica_groups=mesh['fsdp'=16,'model'=8] {'fsdp','model'}, use_global_device_ids=true, to_apply=%add | all-reduce | flops 5120 | bytes 20480
  93.7 25.5 %all-gather.2.cloned.1.call-done = bf16[5120,1280]{1,0:T(8,128)(2,1)} async-done(((bf16[320,1280]{1,0:T(8,128)(2,1)}), bf16[5120,1280]{1,0:T(8,128)(2,1)}) %all-gather.2.cloned.1.call-update) | async-done | bytes 13107216 | tf_op jit(solution)/shard_map/all_gather | solution.py:31
  119.1 3.4 %fusion.3 = (bf16[5120,128]{1,0:T(8,128)(2,1)}, bf16[5120,128]{1,0:T(8,128)(2,1)}) fusion(bf16[5120,1280]{1,0:T(8,128)(2,1)} %all-gather.2.cloned.1.call-done), kind=kLoop, calls=%fused_computation.15 | loop fusion | bytes 5242880 | tf_op jit(solution)/shard_map/split | solution.py:32
  122.5 9.3 %split.12 = bf16[5120,1024]{1,0:T(8,128)(2,1)} slice(bf16[5120,1280]{1,0:T(8,128)(2,1)} %all-gather.2.cloned.1.call-done), slice={[0:5120], [0:1024]} | slice | bytes 20971520 | tf_op jit(solution)/shard_map/split | solution.py:32
  (21 shorter events, 0.1 us)
Async XLA Ops:
  7.2 0.8 copy-start
  7.2 2.3 %copy-start.1 = (bf16[320,128]{1,0:T(8,128)(2,1)S(1)}, bf16[320,128]{1,0:T(8,128)(2,1)}, u32[]{:S(2)}) copy-start(bf16[320,128]{1,0:T(8,128)(2,1)} %param.17) | copy-start | bytes 245764
  7.2 2.3 %copy-start.3 = (bf16[320,32]{0,1:T(8,128)(2,1)S(1)}, bf16[320,32]{0,1:T(8,128)(2,1)}, u32[]{:S(2)}) copy-start(bf16[320,32]{0,1:T(8,128)(2,1)} %param.18) | copy-start | bytes 61444
  7.2 2.3 %copy-start.6 = (bf16[32,128]{1,0:T(8,128)(2,1)S(1)}, bf16[32,128]{1,0:T(8,128)(2,1)}, u32[]{:S(2)}) copy-start(bf16[32,128]{1,0:T(8,128)(2,1)} %param.19) | copy-start | bytes 24580
  7.2 2.5 %copy-start.2 = (bf16[320,128]{1,0:T(8,128)(2,1)S(1)}, bf16[320,128]{1,0:T(8,128)(2,1)}, u32[]{:S(2)}) copy-start(bf16[320,128]{1,0:T(8,128)(2,1)} %param.14) | copy-start | bytes 245764
  7.2 2.5 %copy-start.4 = (bf16[320,32]{0,1:T(8,128)(2,1)S(1)}, bf16[320,32]{0,1:T(8,128)(2,1)}, u32[]{:S(2)}) copy-start(bf16[320,32]{0,1:T(8,128)(2,1)} %param.15) | copy-start | bytes 61444
  7.2 2.5 %copy-start.7 = (bf16[32,128]{1,0:T(8,128)(2,1)S(1)}, bf16[32,128]{1,0:T(8,128)(2,1)}, u32[]{:S(2)}) copy-start(bf16[32,128]{1,0:T(8,128)(2,1)} %param.16) | copy-start | bytes 24580
  7.2 111.9 %all-gather.2.cloned.1.call-start = ((), (), s32[]{:S(2)}) async-start(), calls=%async_computation.1 | async-start | bytes 13926400 | tf_op jit(solution)/shard_map/all_gather | solution.py:31
  24.9 1.2 copy-start.8
  25.0 1.2 copy-start.9
  25.0 1.2 copy-start.5
  25.2 1.0 copy-start.10
  25.2 1.0 copy-start.11
Sparse Core Ops, SparseCore 0:
  26.3 92.7 all-gather.1
where the time goes:
time: 139 us
  blocking collectives  82 us (59%)
  waiting for transfers between devices  25.5 us (18%)
  between operations  14.3 us (10%)
  local copies, waits for them, and re-layouts  13.8 us (10%)
  matrix products  1.9 us (1%)
    unnamed x1, blocking collectives  67.2 us
    all_gather x1, waiting for transfers between devices, sent_together(): out = lax.all_gather(both, axis, axis=dim, tiled=True)  25.5 us
    all_to_all x1, blocking collectives, copy_for_each(): return lax.all_to_all(copies, axis, split_axis=0, concat_axis=0, tiled=True)  14.8 us
    split x2, local copies, waits for them, and re-layouts, sent_together(): jnp.split(out, [sum(widths[:k]) for k in range(1, len(widths))], axis=along)  12.7 us
  transfers between devices with their start and end apart: 1, of which 1 were waited for; matrix products, arithmetic and copies ran while one was open for 0% of the time, Pallas kernels for 0%

commit v1 on v0

v1 whole, which is shorter than its diff:
```python
import jax
import jax.numpy as jnp
from jax import lax
from jax.experimental import pallas as pl
from jax.experimental.pallas import tpu as pltpu
from jax.sharding import PartitionSpec as P


mix_rate = 0.5
SIDE = 4
LANES = 128


def x_ring(step):
    return [(z * SIDE + x, z * SIDE + (x + step) % SIDE) for z in range(SIDE) for x in range(SIDE)]


def z_ring(step):
    return [(z * SIDE + x, (z + step) % SIDE * SIDE + x) for z in range(SIDE) for x in range(SIDE)]


RING = {"x": x_ring, "z": z_ring}


def wrapped(offset):
    return (offset + 1) % SIDE - 1


WAYS = [("x", 1), ("x", -1), ("z", 1), ("z", -1)]
LEAD = {"x": 0, "z": 1}
OTHER = {"x": "z", "z": "x"}
QUARTER = {1: 0, -1: 1}


def sent(array, axis, step):
    return lax.ppermute(array, "fsdp", RING[axis](step))


def all_ways(message):
    return {(ax, s): sent(message(ax, s), ax, s) for ax, s in WAYS}


def shifted(place, axis, step):
    ox, oz, h, k = place
    return (wrapped(ox - step), oz, h, k) if axis == "x" else (ox, wrapped(oz - step), h, k)


def pair(half, axis=None, step=0):
    places = [(0, 0, half, 0), (0, 0, half, 1)]
    return [shifted(p, axis, step) for p in places] if axis else places


def a_places(ax, s):
    return pair(LEAD[ax], ax, s)


def b_places(ax, s):
    return pair(1 - LEAD[ax], ax, s)


def c_message_places(ax, s):
    o = OTHER[ax]
    return [a_places(ax, s)[QUARTER[s]], *a_places(o, 1), *a_places(o, -1)]


def c_places(ax, s):
    return [shifted(p, ax, s) for p in c_message_places(ax, s)]


def d_places(ax, s):
    return [shifted(b_places(ax, s)[QUARTER[s]], ax, s)]


def e_message_places(ax):
    o = OTHER[ax]
    return [c_places(o, 1)[0], c_places(o, -1)[0]]


def e_places(ax, s):
    return [shifted(p, ax, s) for p in e_message_places(ax)]


def f_places(ax, s):
    held, q = c_places(ax, s), QUARTER[s]
    return [shifted(held[1 + q], ax, s), shifted(held[3 + q], ax, s)]


def g_places(ax, s):
    return [shifted(e_places(ax, s)[QUARTER[s]], ax, s)]


HBM = pl.BlockSpec(memory_space=pl.ANY)
VMEM = pl.BlockSpec(memory_space=pltpu.VMEM)


def in_vmem(array):
    return pltpu.with_memory_space_constraint(array, pltpu.VMEM)


def row_of(place, unit):
    me = lax.axis_index("fsdp")
    z, x = me // SIDE, me % SIDE
    ox, oz, h, k = place
    source = (z + oz + SIDE) % SIDE * SIDE + (x + ox + SIDE) % SIDE
    return pl.multiple_of((source * 4 + h * 2 + k) * unit, unit)


def runs(places):
    out, at = [], 0
    while at < len(places):
        ox, oz, h, k = places[at]
        size = 2 if k == 0 and at + 1 < len(places) and places[at + 1] == (ox, oz, h, 1) else 1
        out.append((at, size, places[at]))
        at += size
    return out


def column_copies(ref, first, rows, results, row, widths, sems):
    at = 0
    for n, width in enumerate(widths):
        pltpu.make_async_copy(
            ref.at[pl.ds(first, rows), pl.ds(at, width)], results[n].at[pl.ds(row, rows), :], sems.at[n]
        ).start()
        at += width


def wait_for(rows, results, sems):
    for n, result in enumerate(results):
        part = result.at[pl.ds(0, rows), :]
        pltpu.make_async_copy(part, part, sems.at[n]).wait()


def merged_into(raw, first, rows, mixed_ref, inverse_ref, targets, wide):
    low = raw[pl.ds(first, rows), pl.ds(wide, LANES)]
    tile = 2 * LANES
    for t in range(0, wide, tile):
        update = jnp.dot(low, mixed_ref[:, t : t + tile], preferred_element_type=jnp.float32)
        value = (raw[pl.ds(first, rows), t : t + tile].astype(jnp.float32) + update) * inverse_ref[:, t : t + tile]
        value = value.astype(jnp.bfloat16)
        for ref, at, skip, size in targets:
            ref[pl.ds(at, size), t : t + tile] = value[skip : skip + size]


def first_hop(a, unit, mixed, inverse, widths):
    wide, total = sum(widths), 4 * SIDE * SIDE * unit
    order = {way: n for n, way in enumerate(WAYS)}

    def body(*refs):
        mixed_ref, inverse_ref, raws = refs[0], refs[1], refs[2:6]
        messages, results, sems = refs[6:10], refs[10 : 10 + len(widths)], refs[-1]
        for ax, s in WAYS:
            o, q = OTHER[ax], QUARTER[s]
            at = (1 + 2 * q) * unit
            targets = [
                (messages[order[ax, s]], 0, q * unit, unit),
                (messages[order[o, 1]], at, 0, 2 * unit),
                (messages[order[o, -1]], at, 0, 2 * unit),
            ]
            merged_into(raws[order[ax, s]], 0, 2 * unit, mixed_ref, inverse_ref, targets, wide)
            column_copies(
                messages[order[o, 1]], at, 2 * unit, results, row_of(a_places(ax, s)[0], unit), widths, sems
            )
        wait_for(8 * unit, results, sems)

    out = pl.pallas_call(
        body,
        out_shape=[jax.ShapeDtypeStruct((5 * unit, wide), jnp.bfloat16)] * 4
        + [jax.ShapeDtypeStruct((total, width), jnp.bfloat16) for width in widths],
        in_specs=[VMEM] * 6,
        out_specs=[VMEM] * 4 + [HBM] * len(widths),
        scratch_shapes=[pltpu.SemaphoreType.DMA((len(widths),))],
        compiler_params=pltpu.CompilerParams(vmem_limit_bytes=20 * 2**20),
        name="first_hop",
    )(mixed, inverse, *[in_vmem(a[way]) for way in WAYS])
    return {way: out[n] for n, way in enumerate(WAYS)}, out[4:]


def second_hop(b, own, unit, mixed, inverse, finals, widths):
    wide = sum(widths)

    def body(*refs):
        mixed_ref, inverse_ref, raws, own_ref = refs[0], refs[1], refs[2:6], refs[6]
        messages = refs[7 + len(widths) : 11 + len(widths)]
        results, stage, sems = refs[11 + len(widths) : -2], refs[-2], refs[-1]
        for n, (ax, s) in enumerate(WAYS):
            q = QUARTER[s]
            at = 2 * n * unit
            targets = [(messages[n], 0, q * unit, unit), (stage, at, 0, 2 * unit)]
            merged_into(raws[n], 0, 2 * unit, mixed_ref, inverse_ref, targets, wide)
            column_copies(stage, at, 2 * unit, results, row_of(b_places(ax, s)[0], unit), widths, sems)
        for h in (0, 1):
            at = (8 + 2 * h) * unit
            merged_into(own_ref, 2 * h * unit, 2 * unit, mixed_ref, inverse_ref, [(stage, at, 0, 2 * unit)], wide)
            column_copies(stage, at, 2 * unit, results, row_of((0, 0, h, 0), unit), widths, sems)
        wait_for(12 * unit, results, sems)

    out = pl.pallas_call(
        body,
        out_shape=[jax.ShapeDtypeStruct((unit, wide), jnp.bfloat16)] * 4
        + [jax.ShapeDtypeStruct(f.shape, f.dtype) for f in finals],
        in_specs=[VMEM] * 7 + [HBM] * len(widths),
        out_specs=[VMEM] * 4 + [HBM] * len(widths),
        scratch_shapes=[pltpu.VMEM((12 * unit, wide), jnp.bfloat16), pltpu.SemaphoreType.DMA((len(widths),))],
        input_output_aliases={7 + n: 4 + n for n in range(len(widths))},
        compiler_params=pltpu.CompilerParams(vmem_limit_bytes=20 * 2**20),
        name="second_hop",
    )(mixed, inverse, *[in_vmem(b[way]) for way in WAYS], in_vmem(own), *finals)
    return {way: out[n] for n, way in enumerate(WAYS)}, out[4:]


def placed(groups, unit, finals, widths):
    arrays = [array for array, _ in groups]
    count = len(arrays)

    def body(*refs):
        results, sems = refs[-1 - len(widths) : -1], refs[-1]
        rows = 0
        for ref, (_, places) in zip(refs[:count], groups):
            for at, size, place in runs(places):
                column_copies(ref, at * unit, size * unit, results, row_of(place, unit), widths, sems)
            rows += len(places) * unit
        wait_for(rows, results, sems)

    return pl.pallas_call(
        body,
        out_shape=[jax.ShapeDtypeStruct(f.shape, f.dtype) for f in finals],
        in_specs=[VMEM] * count + [HBM] * len(widths),
        out_specs=[HBM] * len(widths),
        scratch_shapes=[pltpu.SemaphoreType.DMA((len(widths),))],
        input_output_aliases={count + n: n for n in range(len(widths))},
        compiler_params=pltpu.CompilerParams(vmem_limit_bytes=8 * 2**20),
    )(*[in_vmem(array) for array in arrays], *finals)


def round_of_max(values, ring):
    others = []
    for step in (2, 1, -1):
        others.append(lax.ppermute(values, "fsdp", ring(step)))
    return jnp.maximum(jnp.maximum(values, others[0]), jnp.maximum(others[1], others[2]))


def per_device(
    weight_query,
    low_query,
    high_query,
    weight_key,
    low_key,
    high_key,
    weight_value,
    low_value,
    high_value,
    norm_train,
    norm_step,
):
    me = lax.axis_index("fsdp")
    lane = lax.axis_index("model")
    groups, lanes = lax.axis_size("fsdp"), lax.axis_size("model")
    weights = (weight_query, weight_key, weight_value)
    lows = (low_query, low_key, low_value)
    highs = (high_query, high_key, high_value)
    widths = [w.shape[1] for w in weights]
    wide, ranks = sum(widths), [low.shape[1] for low in lows]
    rows = weight_query.shape[0]
    unit = rows // 4
    rest = LANES - sum(ranks)
    block = jnp.concatenate([*weights, *lows, jnp.zeros((rows, rest), jnp.bfloat16)], axis=1)
    halves = [block[: 2 * unit], block[2 * unit :]]
    a = all_ways(lambda ax, s: halves[LEAD[ax]])
    b = all_ways(lambda ax, s: halves[1 - LEAD[ax]])

    largest = [
        jnp.max(
            jnp.abs(w.astype(jnp.float32) + mix_rate * jnp.dot(low, high, preferred_element_type=jnp.float32)),
            axis=0,
        )
        for w, low, high in zip(weights, lows, highs)
    ]
    norm = (norm_train + norm_step).astype(jnp.bfloat16).astype(jnp.float32)
    slots = jnp.where(jnp.arange(groups)[:, None] == me, norm[None, :], -jnp.inf).reshape(-1)
    shared = round_of_max(jnp.concatenate([*largest, slots]), z_ring)
    shared = round_of_max(shared, x_ring)
    columns, at = [], 0
    for width in widths:
        columns.append(shared[at : at + width])
        at += width
    inverse = (1.0 / shared[:wide]).reshape(1, wide)
    mixed, at = [], 0
    for high, width in zip(highs, widths):
        mixed.append(jnp.pad(mix_rate * high, ((0, 0), (at, wide - at - width))))
        at += width
    mixed = jnp.concatenate([*mixed, jnp.zeros((rest, wide), jnp.bfloat16)], axis=0)

    messages, finals = first_hop(a, unit, mixed, inverse, widths)
    c = all_ways(lambda ax, s: messages[ax, s])
    messages, finals = second_hop(b, block, unit, mixed, inverse, finals, widths)
    d = all_ways(lambda ax, s: messages[ax, s])

    mine = shared[wide:].astype(jnp.bfloat16).reshape(groups, 1, -1)
    gains = jnp.where((jnp.arange(lanes) == lane)[None, :, None], mine, -jnp.inf).reshape(-1)
    for n in range(3):
        gains = jnp.maximum(gains, lax.ppermute(gains, "model", [(i, i ^ 2**n) for i in range(lanes)]))

    along = {ax: jnp.concatenate([c[OTHER[ax], 1][:unit], c[OTHER[ax], -1][:unit]]) for ax in "xz"}
    e = all_ways(lambda ax, s: along[ax])

    def forwarded(ax, s):
        held, q = c[ax, s], QUARTER[s]
        return jnp.concatenate([held[(1 + q) * unit : (2 + q) * unit], held[(3 + q) * unit : (4 + q) * unit]])

    f = all_ways(forwarded)
    g = all_ways(lambda ax, s: e[ax, s][QUARTER[s] * unit : (QUARTER[s] + 1) * unit])
    finals = placed([(d[w], d_places(*w)) for w in WAYS], unit, finals, widths)
    finals = placed([(c[w], c_places(*w)) for w in WAYS], unit, finals, widths)
    finals = placed([(e[w], e_places(*w)) for w in WAYS] + [(f[w], f_places(*w)) for w in WAYS], unit, finals, widths)
    finals = placed([(g[w], g_places(*w)) for w in WAYS], unit, finals, widths)
    return (*finals, *columns, gains)


def solution(mesh):
    return jax.shard_map(
        per_device,
        mesh=mesh,
        in_specs=(
            P("fsdp", "model"),
            P("fsdp", None),
            P(None, "model"),
            P("fsdp", "model"),
            P("fsdp", None),
            P(None, "model"),
            P("fsdp", "model"),
            P("fsdp", None),
            P(None, "model"),
            P(("fsdp", "model")),
            P(("fsdp", "model")),
        ),
        out_specs=(
            P(None, "model"),
            P(None, "model"),
            P(None, "model"),
            P("model"),
            P("model"),
            P("model"),
            P(),
        ),
        check_vma=False,
    )
```

time: 139 us -> 144 us (1.036)
  the two profiles are of different devices: /device:TPU:1 before, /device:TPU:0 now
where the time goes in v1:
time: 144 us
  waiting for transfers between devices  74 us (51%)
  starting transfers between devices  47.2 us (33%)
  Pallas kernels  10.8 us (8%)
  local copies, waits for them, and re-layouts  6.31 us (4%)
  matrix products  1.95 us (1%)
  other arithmetic  1.89 us (1%)
    ppermute x28, waiting for transfers between devices, sent(): return lax.ppermute(array, 'fsdp', RING[axis](step))  63.2 us
    ppermute x28, starting transfers between devices, sent(): return lax.ppermute(array, 'fsdp', RING[axis](step))  30.9 us
    ppermute x6, starting transfers between devices, round_of_max(): others.append(lax.ppermute(values, 'fsdp', ring(step)))  11.5 us
    ppermute x6, waiting for transfers between devices, round_of_max(): others.append(lax.ppermute(values, 'fsdp', ring(step)))  9.61 us
    pallas_call x4, Pallas kernels, placed(): pl.pallas_call(body, out_shape=[jax.ShapeDtypeStruct(f.shape, f.dtype) fo...  5.54 us
    ppermute x3, starting transfers between devices, per_device(): lax.ppermute(gains, 'model', [(i, i ^ 2 ** n) for i in range(lanes)])  4.86 us
    unnamed x33, local copies, waits for them, and re-layouts  3.35 us
  transfers between devices with their start and end apart: 37, of which 12 were waited for; matrix products, arithmetic and copies ran while one was open for 3% of the time, Pallas kernels for 5%

profile of v1, /device:TPU:0, one launch (start us, length us, event | category | flops | bytes accessed | tf_op | source)
XLA Modules:
  0.0 143.5 jit_solution(2345288462535499064)
XLA Ops:
  3.7 4.1 %collective-permute-start = (f32[1920]{0:T(1024)S(1)}, f32[1920]{0:T(1024)S(1)}, u32[]{:S(2)}, u32[]{:S(2)}) collective-permute-start(f32[1920]{0:T(1024)S(1)} %pad_maximum_fusion.6), channel_id=1, source_target_pairs={{0,64},{8,72},{16,80},{24,88},{32,96},{40,104},{48,112},{56,120},{... | collective-permute-start | bytes 23048 | tf_op jit(solution)/shard_map/ppermute | solution.py:238
  8.8 2.2 %collective-permute-start.2 = (f32[1920]{0:T(1024)S(1)}, f32[1920]{0:T(1024)S(1)}, u32[]{:S(2)}, u32[]{:S(2)}) collective-permute-start(f32[1920]{0:T(1024)S(1)} %pad_maximum_fusion.6), channel_id=1, source_target_pairs={{0,96},{8,104},{16,112},{24,120},{32,0},{40,8},{48,16},{56,24},{64... | collective-permute-start | bytes 23048 | tf_op jit(solution)/shard_map/ppermute | solution.py:238
  16.1 1.9 %collective-permute-start.3 = (f32[1920]{0:T(1024)S(1)}, f32[1920]{0:T(1024)S(1)}, u32[]{:S(2)}, u32[]{:S(2)}) collective-permute-start(f32[1920]{0:T(1024)S(1)} %maximum_maximum_fusion.1), channel_id=1, source_target_pairs={{0,16},{8,24},{16,0},{24,8},{32,48},{40,56},{48,32},{56,40},{64,80... | collective-permute-start | bytes 23048 | tf_op jit(solution)/shard_map/ppermute | solution.py:238
  18.6 7.8 %collective-permute-done.3 = f32[1920]{0:T(1024)S(1)} collective-permute-done((f32[1920]{0:T(1024)S(1)}, f32[1920]{0:T(1024)S(1)}, u32[]{:S(2)}, u32[]{:S(2)}) %collective-permute-start.3) | collective-permute-done | bytes 7712 | tf_op jit(solution)/shard_map/ppermute | solution.py:238
  28.5 1.8 %collective-permute-done.5 = f32[1920]{0:T(1024)S(1)} collective-permute-done((f32[1920]{0:T(1024)S(1)}, f32[1920]{0:T(1024)S(1)}, u32[]{:S(2)}, u32[]{:S(2)}) %collective-permute-start.5) | collective-permute-done | bytes 7712 | tf_op jit(solution)/shard_map/ppermute | solution.py:238
  30.4 6.2 %collective-permute-done.9.refs_5_ = bf16[160,1408]{1,0:T(8,128)(2,1)S(1)} collective-permute-done((bf16[160,1408]{1,0:T(8,128)(2,1)}, bf16[160,1408]{1,0:T(8,128)(2,1)S(1)}, u32[]{:S(2)}, u32[]{:S(2)}) %collective-permute-start.9) | collective-permute-done | bytes 450592 | tf_op jit(solution)/shard_map/ppermute | solution.py:36
  36.6 2.4 %first_hop.1 = (bf16[400,1280]{1,0:T(8,128)(2,1)S(1)}, bf16[400,1280]{1,0:T(8,128)(2,1)}, bf16[400,1280]{1,0:T(8,128)(2,1)S(1)}, bf16[400,1280]{1,0:T(8,128)(2,1...) custom-call(bf16[128,1280]{1,0:T(8,128)(2,1)S(1)} %fusion.15.refs_0_, ...), custom_call_target="tpu_custom_call" | custom-call | tf_op jit(solution)/shard_map/first_hop/pallas_call | solution.py:165
  48.4 2.1 %collective-permute-start.27 = (bf16[160,1408]{1,0:T(8,128)(2,1)}, bf16[160,1408]{1,0:T(8,128)(2,1)S(1)}, u32[]{:S(2)}, u32[]{:S(2)}) collective-permute-start(bf16[160,1408]{1,0:T(8,128)(2,1)} %get-tuple-element.71), channel_id=1, source_target_pairs={{0,24},{8,0},{16,8},{24,16},{32,56},{40,32},{48,40},{56,48},{64,88... | collective-permute-start | bytes 1351688 | tf_op jit(solution)/shard_map/ppermute | solution.py:36
  50.5 7.7 %collective-permute-done.26.refs_2_ = bf16[160,1408]{1,0:T(8,128)(2,1)} collective-permute-done((bf16[160,1408]{1,0:T(8,128)(2,1)}, bf16[160,1408]{1,0:T(8,128)(2,1)}, u32[]{:S(2)}, u32[]{:S(2)}) %collective-permute-start.26) | collective-permute-done | bytes 450592 | tf_op jit(solution)/shard_map/ppermute | solution.py:36
  59.9 13.4 %collective-permute-done.27.refs_3_ = bf16[160,1408]{1,0:T(8,128)(2,1)S(1)} collective-permute-done((bf16[160,1408]{1,0:T(8,128)(2,1)}, bf16[160,1408]{1,0:T(8,128)(2,1)S(1)}, u32[]{:S(2)}, u32[]{:S(2)}) %collective-permute-start.27) | collective-permute-done | bytes 450592 | tf_op jit(solution)/shard_map/ppermute | solution.py:36
  73.3 3.2 %collective-permute-start.36 = (bf16[5120]{0:T(1024)(128)(2,1)S(1)}, bf16[5120]{0:T(1024)(128)(2,1)S(1)}, u32[]{:S(2)}, u32[]{:S(2)}) collective-permute-start(bf16[5120]{0:T(1024)(128)(2,1)S(1)} %max.34), channel_id=1, source_target_pairs={{0,4},{1,5},{2,6},{3,7},{4,0},{5,1},{6,2},{7,3},{8,12},{9,13},{10,... | collective-permute-start | bytes 30728 | tf_op jit(solution)/shard_map/ppermute | solution.py:301
  76.5 2.9 %second_hop.1 = (bf16[80,1280]{1,0:T(8,128)(2,1)S(1)}, bf16[80,1280]{1,0:T(8,128)(2,1)S(1)}, bf16[80,1280]{1,0:T(8,128)(2,1)S(1)}, bf16[80,1280]{1,0:T(8,128)(2,...) custom-call(bf16[128,1280]{1,0:T(8,128)(2,1)S(1)} %fusion.15.refs_0_, ...), custom_call_target="tpu_custom_call", output_to_operand_aliasing={{4}: (7, {}), {5}: (8, {}), {6}: (9, {})} | custom-call | tf_op jit(solution)/shard_map/second_hop/pallas_call | solution.py:197
  80.7 2.0 %collective-permute-start.31 = (bf16[80,1280]{1,0:T(8,128)(2,1)S(1)}, bf16[80,1280]{1,0:T(8,128)(2,1)S(1)}, u32[]{:S(2)}, u32[]{:S(2)}) collective-permute-start(bf16[80,1280]{1,0:T(8,128)(2,1)S(1)} %get-tuple-element.41), channel_id=1, source_target_pairs={{0,24},{8,0},{16,8},{24,16},{32,56},{40,32},{48,40},{56,48},{64,88... | collective-permute-start | bytes 614408 | tf_op jit(solution)/shard_map/ppermute | solution.py:36
  82.7 2.1 %collective-permute-start.11 = (bf16[400,1280]{1,0:T(8,128)(2,1)S(1)}, bf16[400,1280]{1,0:T(8,128)(2,1)S(1)}, u32[]{:S(2)}, u32[]{:S(2)}) collective-permute-start(bf16[400,1280]{1,0:T(8,128)(2,1)S(1)} %copy-done.3), channel_id=1, source_target_pairs={{0,96},{8,104},{16,112},{24,120},{32,0},{40,8},{48,16},{56,24},{64... | collective-permute-start | bytes 3072008 | tf_op jit(solution)/shard_map/ppermute | solution.py:36
  85.0 18.7 %collective-permute-done.11.refs_3_ = bf16[400,1280]{1,0:T(8,128)(2,1)S(1)} collective-permute-done((bf16[400,1280]{1,0:T(8,128)(2,1)S(1)}, bf16[400,1280]{1,0:T(8,128)(2,1)S(1)}, u32[]{:S(2)}, u32[]{:S(2)}) %collective-permute-start.11) | collective-permute-done | bytes 1024032 | tf_op jit(solution)/shard_map/ppermute | solution.py:36
  103.8 6.4 %collective-permute-done.10.refs_2_ = bf16[400,1280]{1,0:T(8,128)(2,1)S(1)} collective-permute-done((bf16[400,1280]{1,0:T(8,128)(2,1)S(1)}, bf16[400,1280]{1,0:T(8,128)(2,1)S(1)}, u32[]{:S(2)}, u32[]{:S(2)}) %collective-permute-start.10) | collective-permute-done | bytes 1024032 | tf_op jit(solution)/shard_map/ppermute | solution.py:36
  110.6 2.1 %collective-permute-start.32 = (bf16[80,1280]{1,0:T(8,128)(2,1)S(1)}, bf16[80,1280]{1,0:T(8,128)(2,1)S(1)}, u32[]{:S(2)}, u32[]{:S(2)}) collective-permute-start(bf16[80,1280]{1,0:T(8,128)(2,1)S(1)} %get-tuple-element.42), channel_id=1, source_target_pairs={{0,32},{8,40},{16,48},{24,56},{32,64},{40,72},{48,80},{56,88},{64,... | collective-permute-start | bytes 614408 | tf_op jit(solution)/shard_map/ppermute | solution.py:36
  112.7 3.2 %collective-permute-start.14 = (bf16[160,1280]{1,0:T(8,128)(2,1)S(1)}, bf16[160,1280]{1,0:T(8,128)(2,1)S(1)}, u32[]{:S(2)}, u32[]{:S(2)}) collective-permute-start(bf16[160,1280]{1,0:T(8,128)(2,1)S(1)} %pad_maximum_fusion), channel_id=1, source_target_pairs={{0,24},{8,0},{16,8},{24,16},{32,56},{40,32},{48,40},{56,48},{64,88... | collective-permute-start | bytes 1228808 | tf_op jit(solution)/shard_map/ppermute | solution.py:36
  116.0 3.4 %collective-permute-done.32.refs_2_ = bf16[80,1280]{1,0:T(8,128)(2,1)S(1)} collective-permute-done((bf16[80,1280]{1,0:T(8,128)(2,1)S(1)}, bf16[80,1280]{1,0:T(8,128)(2,1)S(1)}, u32[]{:S(2)}, u32[]{:S(2)}) %collective-permute-start.32) | collective-permute-done | bytes 204832 | tf_op jit(solution)/shard_map/ppermute | solution.py:36
  119.4 2.1 %collective-permute-start.24 = (bf16[160,1280]{1,0:T(8,128)(2,1)S(1)}, bf16[160,1280]{1,0:T(8,128)(2,1)S(1)}, u32[]{:S(2)}, u32[]{:S(2)}) collective-permute-start(bf16[160,1280]{1,0:T(8,128)(2,1)S(1)} %pad_maximum_fusion.4), channel_id=1, source_target_pairs={{0,32},{8,40},{16,48},{24,56},{32,64},{40,72},{48,80},{56,88},{64,... | collective-permute-start | bytes 1228808 | tf_op jit(solution)/shard_map/ppermute | solution.py:36
  121.5 3.2 %collective-permute-start.23 = (bf16[160,1280]{1,0:T(8,128)(2,1)S(1)}, bf16[160,1280]{1,0:T(8,128)(2,1)S(1)}, u32[]{:S(2)}, u32[]{:S(2)}) collective-permute-start(bf16[160,1280]{1,0:T(8,128)(2,1)S(1)} %pad_maximum_fusion.3), channel_id=1, source_target_pairs={{0,24},{8,0},{16,8},{24,16},{32,56},{40,32},{48,40},{56,48},{64,88... | collective-permute-start | bytes 1228808 | tf_op jit(solution)/shard_map/ppermute | solution.py:36
  127.6 5.8 %collective-permute-done.25.refs_7_ = bf16[160,1280]{1,0:T(8,128)(2,1)S(1)} collective-permute-done((bf16[160,1280]{1,0:T(8,128)(2,1)S(1)}, bf16[160,1280]{1,0:T(8,128)(2,1)S(1)}, u32[]{:S(2)}, u32[]{:S(2)}) %collective-permute-start.25) | collective-permute-done | bytes 409632 | tf_op jit(solution)/shard_map/ppermute | solution.py:36
  133.4 3.2 %collective-permute-start.15 = (bf16[80,1280]{1,0:T(8,128)(2,1)S(1)}, bf16[80,1280]{1,0:T(8,128)(2,1)S(1)}, u32[]{:S(2)}, u32[]{:S(2)}) collective-permute-start(bf16[80,1280]{1,0:T(8,128)(2,1)S(1)} %slice.107), channel_id=1, source_target_pairs={{0,24},{8,0},{16,8},{24,16},{32,56},{40,32},{48,40},{56,48},{64,88... | collective-permute-start | bytes 614408 | tf_op jit(solution)/shard_map/ppermute | solution.py:36
  138.7 2.0 %shard_map.163 = (bf16[5120,1024]{1,0:T(8,128)(2,1)}, bf16[5120,128]{1,0:T(8,128)(2,1)}, bf16[5120,128]{1,0:T(8,128)(2,1)}) custom-call(bf16[400,1280]{1,0:T(8,128)(2,1)S(1)} %collective-permute-done.16.refs_0_, bf16[400,1280]{1,0:T(8,128)(2,1)S(1)} %collective-permute-done.17.refs_1_, ...), custom_call_target="tpu_custom_call", output_to_operand_aliasing={{0}: (4, {}), {1}: (5, {}), {2}: (6, {})} | custom-call | tf_op jit(solution)/shard_map/pallas_call | solution.py:224
  (133 shorter events, 32.3 us)
Async XLA Ops:
  3.7 12.2 %collective-permute-start = (f32[1920]{0:T(1024)S(1)}, f32[1920]{0:T(1024)S(1)}, u32[]{:S(2)}, u32[]{:S(2)}) collective-permute-start(f32[1920]{0:T(1024)S(1)} %pad_maximum_fusion.6), channel_id=1, source_target_pairs={{0,64},{8,72},{16,80},{24,88},{32,96},{40,104},{48,112},{56,120},{... | collective-permute-start | bytes 23048 | tf_op jit(solution)/shard_map/ppermute | solution.py:238
  12.7 17.7 %collective-permute-start.6 = (bf16[160,1408]{1,0:T(8,128)(2,1)S(1)}, bf16[160,1408]{1,0:T(8,128)(2,1)S(1)}, u32[]{:S(2)}, u32[]{:S(2)}) collective-permute-start(bf16[160,1408]{1,0:T(8,128)(2,1)S(1)} %get-tuple-element.72), channel_id=1, source_target_pairs={{0,8},{8,16},{16,24},{24,0},{32,40},{40,48},{48,56},{56,32},{64,72... | collective-permute-start | bytes 1351688 | tf_op jit(solution)/shard_map/ppermute | solution.py:36
  14.2 16.2 %collective-permute-start.7 = (bf16[160,1408]{1,0:T(8,128)(2,1)S(1)}, bf16[160,1408]{1,0:T(8,128)(2,1)S(1)}, u32[]{:S(2)}, u32[]{:S(2)}) collective-permute-start(bf16[160,1408]{1,0:T(8,128)(2,1)S(1)} %get-tuple-element.72), channel_id=1, source_target_pairs={{0,24},{8,0},{16,8},{24,16},{32,56},{40,32},{48,40},{56,48},{64,88... | collective-permute-start | bytes 1351688 | tf_op jit(solution)/shard_map/ppermute | solution.py:36
  16.0 14.4 %collective-permute-start.8 = (bf16[160,1408]{1,0:T(8,128)(2,1)}, bf16[160,1408]{1,0:T(8,128)(2,1)S(1)}, u32[]{:S(2)}, u32[]{:S(2)}) collective-permute-start(bf16[160,1408]{1,0:T(8,128)(2,1)} %get-tuple-element.71), channel_id=1, source_target_pairs={{0,32},{8,40},{16,48},{24,56},{32,64},{40,72},{48,80},{56,88},{64,... | collective-permute-start | bytes 1351688 | tf_op jit(solution)/shard_map/ppermute | solution.py:36
  16.1 10.3 %collective-permute-start.3 = (f32[1920]{0:T(1024)S(1)}, f32[1920]{0:T(1024)S(1)}, u32[]{:S(2)}, u32[]{:S(2)}) collective-permute-start(f32[1920]{0:T(1024)S(1)} %maximum_maximum_fusion.1), channel_id=1, source_target_pairs={{0,16},{8,24},{16,0},{24,8},{32,48},{40,56},{48,32},{56,40},{64,80... | collective-permute-start | bytes 23048 | tf_op jit(solution)/shard_map/ppermute | solution.py:238
  42.0 40.7 %collective-permute-start.17 = (bf16[400,1280]{1,0:T(8,128)(2,1)}, bf16[400,1280]{1,0:T(8,128)(2,1)S(1)}, u32[]{:S(2)}, u32[]{:S(2)}) collective-permute-start(bf16[400,1280]{1,0:T(8,128)(2,1)} %get-tuple-element.36), channel_id=1, source_target_pairs={{0,24},{8,0},{16,8},{24,16},{32,56},{40,32},{48,40},{56,48},{64,88... | collective-permute-start | bytes 3072008 | tf_op jit(solution)/shard_map/ppermute | solution.py:36
  43.4 14.7 %collective-permute-start.26 = (bf16[160,1408]{1,0:T(8,128)(2,1)}, bf16[160,1408]{1,0:T(8,128)(2,1)}, u32[]{:S(2)}, u32[]{:S(2)}) collective-permute-start(bf16[160,1408]{1,0:T(8,128)(2,1)} %get-tuple-element.71), channel_id=1, source_target_pairs={{0,8},{8,16},{16,24},{24,0},{32,40},{40,48},{48,56},{56,32},{64,72... | collective-permute-start | bytes 1351688 | tf_op jit(solution)/shard_map/ppermute | solution.py:36
  44.1 40.7 %collective-permute-start.16 = (bf16[400,1280]{1,0:T(8,128)(2,1)}, bf16[400,1280]{1,0:T(8,128)(2,1)S(1)}, u32[]{:S(2)}, u32[]{:S(2)}) collective-permute-start(bf16[400,1280]{1,0:T(8,128)(2,1)} %copy-done.4), channel_id=1, source_target_pairs={{0,8},{8,16},{16,24},{24,0},{32,40},{40,48},{48,56},{56,32},{64,72... | collective-permute-start | bytes 3072008 | tf_op jit(solution)/shard_map/ppermute | solution.py:36
  48.4 24.9 %collective-permute-start.27 = (bf16[160,1408]{1,0:T(8,128)(2,1)}, bf16[160,1408]{1,0:T(8,128)(2,1)S(1)}, u32[]{:S(2)}, u32[]{:S(2)}) collective-permute-start(bf16[160,1408]{1,0:T(8,128)(2,1)} %get-tuple-element.71), channel_id=1, source_target_pairs={{0,24},{8,0},{16,8},{24,16},{32,56},{40,32},{48,40},{56,48},{64,88... | collective-permute-start | bytes 1351688 | tf_op jit(solution)/shard_map/ppermute | solution.py:36
  50.5 26.0 %collective-permute-start.28 = (bf16[160,1408]{1,0:T(8,128)(2,1)}, bf16[160,1408]{1,0:T(8,128)(2,1)S(1)}, u32[]{:S(2)}, u32[]{:S(2)}) collective-permute-start(bf16[160,1408]{1,0:T(8,128)(2,1)} %copy-done.6), channel_id=1, source_target_pairs={{0,32},{8,40},{16,48},{24,56},{32,64},{40,72},{48,80},{56,88},{64,... | collective-permute-start | bytes 1351688 | tf_op jit(solution)/shard_map/ppermute | solution.py:36
  58.1 18.4 %collective-permute-start.29 = (bf16[160,1408]{1,0:T(8,128)(2,1)}, bf16[160,1408]{1,0:T(8,128)(2,1)S(1)}, u32[]{:S(2)}, u32[]{:S(2)}) collective-permute-start(bf16[160,1408]{1,0:T(8,128)(2,1)} %copy-done.6), channel_id=1, source_target_pairs={{0,96},{8,104},{16,112},{24,120},{32,0},{40,8},{48,16},{56,24},{64... | collective-permute-start | bytes 1351688 | tf_op jit(solution)/shard_map/ppermute | solution.py:36
  73.3 37.0 %collective-permute-start.36 = (bf16[5120]{0:T(1024)(128)(2,1)S(1)}, bf16[5120]{0:T(1024)(128)(2,1)S(1)}, u32[]{:S(2)}, u32[]{:S(2)}) collective-permute-start(bf16[5120]{0:T(1024)(128)(2,1)S(1)} %max.34), channel_id=1, source_target_pairs={{0,4},{1,5},{2,6},{3,7},{4,0},{5,1},{6,2},{7,3},{8,12},{9,13},{10,... | collective-permute-start | bytes 30728 | tf_op jit(solution)/shard_map/ppermute | solution.py:301
  79.4 31.2 %collective-permute-start.30 = (bf16[80,1280]{1,0:T(8,128)(2,1)S(1)}, bf16[80,1280]{1,0:T(8,128)(2,1)S(1)}, u32[]{:S(2)}, u32[]{:S(2)}) collective-permute-start(bf16[80,1280]{1,0:T(8,128)(2,1)S(1)} %get-tuple-element.40), channel_id=1, source_target_pairs={{0,8},{8,16},{16,24},{24,0},{32,40},{40,48},{48,56},{56,32},{64,72... | collective-permute-start | bytes 614408 | tf_op jit(solution)/shard_map/ppermute | solution.py:36
  80.7 32.0 %collective-permute-start.31 = (bf16[80,1280]{1,0:T(8,128)(2,1)S(1)}, bf16[80,1280]{1,0:T(8,128)(2,1)S(1)}, u32[]{:S(2)}, u32[]{:S(2)}) collective-permute-start(bf16[80,1280]{1,0:T(8,128)(2,1)S(1)} %get-tuple-element.41), channel_id=1, source_target_pairs={{0,24},{8,0},{16,8},{24,16},{32,56},{40,32},{48,40},{56,48},{64,88... | collective-permute-start | bytes 614408 | tf_op jit(solution)/shard_map/ppermute | solution.py:36
  82.7 21.0 %collective-permute-start.11 = (bf16[400,1280]{1,0:T(8,128)(2,1)S(1)}, bf16[400,1280]{1,0:T(8,128)(2,1)S(1)}, u32[]{:S(2)}, u32[]{:S(2)}) collective-permute-start(bf16[400,1280]{1,0:T(8,128)(2,1)S(1)} %copy-done.3), channel_id=1, source_target_pairs={{0,96},{8,104},{16,112},{24,120},{32,0},{40,8},{48,16},{56,24},{64... | collective-permute-start | bytes 3072008 | tf_op jit(solution)/shard_map/ppermute | solution.py:36
  84.8 25.4 %collective-permute-start.10 = (bf16[400,1280]{1,0:T(8,128)(2,1)S(1)}, bf16[400,1280]{1,0:T(8,128)(2,1)S(1)}, u32[]{:S(2)}, u32[]{:S(2)}) collective-permute-start(bf16[400,1280]{1,0:T(8,128)(2,1)S(1)} %copy-done.1), channel_id=1, source_target_pairs={{0,32},{8,40},{16,48},{24,56},{32,64},{40,72},{48,80},{56,88},{64,... | collective-permute-start | bytes 3072008 | tf_op jit(solution)/shard_map/ppermute | solution.py:36
  103.7 15.7 %collective-permute-start.18 = (bf16[160,1280]{1,0:T(8,128)(2,1)S(1)}, bf16[160,1280]{1,0:T(8,128)(2,1)S(1)}, u32[]{:S(2)}, u32[]{:S(2)}) collective-permute-start(bf16[160,1280]{1,0:T(8,128)(2,1)S(1)} %pad_maximum_fusion.1), channel_id=1, source_target_pairs={{0,32},{8,40},{16,48},{24,56},{32,64},{40,72},{48,80},{56,88},{64,... | collective-permute-start | bytes 1228808 | tf_op jit(solution)/shard_map/ppermute | solution.py:36
  110.3 11.2 %collective-permute-start.12 = (bf16[160,1280]{1,0:T(8,128)(2,1)S(1)}, bf16[160,1280]{1,0:T(8,128)(2,1)S(1)}, u32[]{:S(2)}, u32[]{:S(2)}) collective-permute-start(bf16[160,1280]{1,0:T(8,128)(2,1)S(1)} %pad_maximum_fusion), channel_id=1, source_target_pairs={{0,8},{8,16},{16,24},{24,0},{32,40},{40,48},{48,56},{56,32},{64,72... | collective-permute-start | bytes 1228808 | tf_op jit(solution)/shard_map/ppermute | solution.py:36
  112.7 13.0 %collective-permute-start.14 = (bf16[160,1280]{1,0:T(8,128)(2,1)S(1)}, bf16[160,1280]{1,0:T(8,128)(2,1)S(1)}, u32[]{:S(2)}, u32[]{:S(2)}) collective-permute-start(bf16[160,1280]{1,0:T(8,128)(2,1)S(1)} %pad_maximum_fusion), channel_id=1, source_target_pairs={{0,24},{8,0},{16,8},{24,16},{32,56},{40,32},{48,40},{56,48},{64,88... | collective-permute-start | bytes 1228808 | tf_op jit(solution)/shard_map/ppermute | solution.py:36
  119.4 14.0 %collective-permute-start.25 = (bf16[160,1280]{1,0:T(8,128)(2,1)S(1)}, bf16[160,1280]{1,0:T(8,128)(2,1)S(1)}, u32[]{:S(2)}, u32[]{:S(2)}) collective-permute-start(bf16[160,1280]{1,0:T(8,128)(2,1)S(1)} %pad_maximum_fusion.5), channel_id=1, source_target_pairs={{0,96},{8,104},{16,112},{24,120},{32,0},{40,8},{48,16},{56,24},{64... | collective-permute-start | bytes 1228808 | tf_op jit(solution)/shard_map/ppermute | solution.py:36
  119.4 14.0 %collective-permute-start.24 = (bf16[160,1280]{1,0:T(8,128)(2,1)S(1)}, bf16[160,1280]{1,0:T(8,128)(2,1)S(1)}, u32[]{:S(2)}, u32[]{:S(2)}) collective-permute-start(bf16[160,1280]{1,0:T(8,128)(2,1)S(1)} %pad_maximum_fusion.4), channel_id=1, source_target_pairs={{0,32},{8,40},{16,48},{24,56},{32,64},{40,72},{48,80},{56,88},{64,... | collective-permute-start | bytes 1228808 | tf_op jit(solution)/shard_map/ppermute | solution.py:36
  121.5 11.9 %collective-permute-start.23 = (bf16[160,1280]{1,0:T(8,128)(2,1)S(1)}, bf16[160,1280]{1,0:T(8,128)(2,1)S(1)}, u32[]{:S(2)}, u32[]{:S(2)}) collective-permute-start(bf16[160,1280]{1,0:T(8,128)(2,1)S(1)} %pad_maximum_fusion.3), channel_id=1, source_target_pairs={{0,24},{8,0},{16,8},{24,16},{32,56},{40,32},{48,40},{56,48},{64,88... | collective-permute-start | bytes 1228808 | tf_op jit(solution)/shard_map/ppermute | solution.py:36
  125.7 15.0 %collective-permute-start.22 = (bf16[160,1280]{1,0:T(8,128)(2,1)S(1)}, bf16[160,1280]{1,0:T(8,128)(2,1)S(1)}, u32[]{:S(2)}, u32[]{:S(2)}) collective-permute-start(bf16[160,1280]{1,0:T(8,128)(2,1)S(1)} %pad_maximum_fusion.2), channel_id=1, source_target_pairs={{0,8},{8,16},{16,24},{24,0},{32,40},{40,48},{48,56},{56,32},{64,72... | collective-permute-start | bytes 1228808 | tf_op jit(solution)/shard_map/ppermute | solution.py:36
  126.9 15.5 %collective-permute-start.19 = (bf16[80,1280]{1,0:T(8,128)(2,1)S(1)}, bf16[80,1280]{1,0:T(8,128)(2,1)S(1)}, u32[]{:S(2)}, u32[]{:S(2)}) collective-permute-start(bf16[80,1280]{1,0:T(8,128)(2,1)S(1)} %slice.110), channel_id=1, source_target_pairs={{0,32},{8,40},{16,48},{24,56},{32,64},{40,72},{48,80},{56,88},{64,... | collective-permute-start | bytes 614408 | tf_op jit(solution)/shard_map/ppermute | solution.py:36
  (28 other events, 172.1 us)

commit v2 on v1

--- a/solution.py
+++ b/solution.py
@@ -169,7 +169,7 @@
         in_specs=[VMEM] * 6,
         out_specs=[VMEM] * 4 + [HBM] * len(widths),
         scratch_shapes=[pltpu.SemaphoreType.DMA((len(widths),))],
-        compiler_params=pltpu.CompilerParams(vmem_limit_bytes=20 * 2**20),
+        compiler_params=pltpu.CompilerParams(vmem_limit_bytes=8 * 2**20),
         name="first_hop",
     )(mixed, inverse, *[in_vmem(a[way]) for way in WAYS])
     return {way: out[n] for n, way in enumerate(WAYS)}, out[4:]
@@ -179,9 +179,9 @@
     wide = sum(widths)
 
     def body(*refs):
-        mixed_ref, inverse_ref, raws, own_ref = refs[0], refs[1], refs[2:6], refs[6]
-        messages = refs[7 + len(widths) : 11 + len(widths)]
-        results, stage, sems = refs[11 + len(widths) : -2], refs[-2], refs[-1]
+        mixed_ref, inverse_ref, raws, own_refs = refs[0], refs[1], refs[2:6], refs[6:8]
+        messages = refs[8 + len(widths) : 12 + len(widths)]
+        results, stage, sems = refs[12 + len(widths) : -2], refs[-2], refs[-1]
         for n, (ax, s) in enumerate(WAYS):
             q = QUARTER[s]
             at = 2 * n * unit
@@ -190,7 +190,7 @@
             column_copies(stage, at, 2 * unit, results, row_of(b_places(ax, s)[0], unit), widths, sems)
         for h in (0, 1):
             at = (8 + 2 * h) * unit
-            merged_into(own_ref, 2 * h * unit, 2 * unit, mixed_ref, inverse_ref, [(stage, at, 0, 2 * unit)], wide)
+            merged_into(own_refs[h], 0, 2 * unit, mixed_ref, inverse_ref, [(stage, at, 0, 2 * unit)], wide)
             column_copies(stage, at, 2 * unit, results, row_of((0, 0, h, 0), unit), widths, sems)
         wait_for(12 * unit, results, sems)
 
@@ -198,13 +198,13 @@
         body,
         out_shape=[jax.ShapeDtypeStruct((unit, wide), jnp.bfloat16)] * 4
         + [jax.ShapeDtypeStruct(f.shape, f.dtype) for f in finals],
-        in_specs=[VMEM] * 7 + [HBM] * len(widths),
+        in_specs=[VMEM] * 8 + [HBM] * len(widths),
         out_specs=[VMEM] * 4 + [HBM] * len(widths),
         scratch_shapes=[pltpu.VMEM((12 * unit, wide), jnp.bfloat16), pltpu.SemaphoreType.DMA((len(widths),))],
-        input_output_aliases={7 + n: 4 + n for n in range(len(widths))},
-        compiler_params=pltpu.CompilerParams(vmem_limit_bytes=20 * 2**20),
+        input_output_aliases={8 + n: 4 + n for n in range(len(widths))},
+        compiler_params=pltpu.CompilerParams(vmem_limit_bytes=8 * 2**20),
         name="second_hop",
-    )(mixed, inverse, *[in_vmem(b[way]) for way in WAYS], in_vmem(own), *finals)
+    )(mixed, inverse, *[in_vmem(b[way]) for way in WAYS], *[in_vmem(half) for half in own], *finals)
     return {way: out[n] for n, way in enumerate(WAYS)}, out[4:]
 
 
@@ -230,6 +230,54 @@
         input_output_aliases={count + n: n for n in range(len(widths))},
         compiler_params=pltpu.CompilerParams(vmem_limit_bytes=8 * 2**20),
     )(*[in_vmem(array) for array in arrays], *finals)
+
+
+def packed(weights, lows, widths):
+    rows, wide = weights[0].shape[0], sum(widths)
+    half, rank, count = rows // 2, lows[0].shape[1], len(weights)
+
+    def body(*refs):
+        sources, turned, outs = refs[:count], refs[count : 2 * count], refs[2 * count : 2 * count + 2]
+        stage, sems = refs[-2], refs[-1]
+        low_copies = [
+            pltpu.make_async_copy(turned[n], stage.at[n], sems.at[n])
+            for n in range(count)
+        ]
+        for copy in low_copies:
+            copy.start()
+        copies, at = [], 0
+        for n, width in enumerate(widths):
+            for h in (0, 1):
+                copies.append(
+                    pltpu.make_async_copy(
+                        sources[n].at[pl.ds(h * half, half), :],
+                        outs[h].at[:, pl.ds(at, width)],
+                        sems.at[count + 2 * n + h],
+                    )
+                )
+                copies[-1].start()
+            at += width
+        for copy in low_copies:
+            copy.wait()
+        low = jnp.concatenate(
+            [stage[n].astype(jnp.float32) for n in range(count)]
+            + [jnp.zeros((LANES - count * rank, rows), jnp.float32)]
+        )
+        straight = low.T.astype(stage.dtype)
+        for h in (0, 1):
+            outs[h][:, wide:] = straight[h * half : (h + 1) * half]
+        for copy in copies:
+            copy.wait()
+
+    return pl.pallas_call(
+        body,
+        out_shape=[jax.ShapeDtypeStruct((half, wide + LANES), jnp.bfloat16)] * 2,
+        in_specs=[pl.BlockSpec(memory_space=pltpu.MemorySpace.HBM)] * (2 * count),
+        out_specs=[VMEM] * 2,
+        scratch_shapes=[pltpu.VMEM((count, rank, rows), jnp.bfloat16), pltpu.SemaphoreType.DMA((3 * count,))],
+        compiler_params=pltpu.CompilerParams(vmem_limit_bytes=4 * 2**20),
+        name="packed",
+    )(*[pltpu.with_memory_space_constraint(a, pltpu.MemorySpace.HBM) for a in (*weights, *[low.T for low in lows])])
 
 
 def round_of_max(values, ring):
@@ -263,8 +311,11 @@
     rows = weight_query.shape[0]
     unit = rows // 4
     rest = LANES - sum(ranks)
-    block = jnp.concatenate([*weights, *lows, jnp.zeros((rows, rest), jnp.bfloat16)], axis=1)
-    halves = [block[: 2 * unit], block[2 * unit :]]
+    norm = (norm_train + norm_step).astype(jnp.bfloat16).astype(jnp.float32)
+    slots = lax.dynamic_update_slice(
+        jnp.full((groups * lanes * norm.shape[0],), -jnp.inf), norm, ((me * lanes + lane) * norm.shape[0],)
+    )
+    halves = packed(weights, lows, widths)
     a = all_ways(lambda ax, s: halves[LEAD[ax]])
     b = all_ways(lambda ax, s: halves[1 - LEAD[ax]])
 
@@ -275,8 +326,6 @@
         )
         for w, low, high in zip(weights, lows, highs)
     ]
-    norm = (norm_train + norm_step).astype(jnp.bfloat16).astype(jnp.float32)
-    slots = jnp.where(jnp.arange(groups)[:, None] == me, norm[None, :], -jnp.inf).reshape(-1)
     shared = round_of_max(jnp.concatenate([*largest, slots]), z_ring)
     shared = round_of_max(shared, x_ring)
     columns, at = [], 0
@@ -292,13 +341,15 @@
 
     messages, finals = first_hop(a, unit, mixed, inverse, widths)
     c = all_ways(lambda ax, s: messages[ax, s])
-    messages, finals = second_hop(b, block, unit, mixed, inverse, finals, widths)
+    messages, finals = second_hop(b, halves, unit, mixed, inverse, finals, widths)
     d = all_ways(lambda ax, s: messages[ax, s])
 
-    mine = shared[wide:].astype(jnp.bfloat16).reshape(groups, 1, -1)
-    gains = jnp.where((jnp.arange(lanes) == lane)[None, :, None], mine, -jnp.inf).reshape(-1)
+    gains = shared[wide:]
     for n in range(3):
-        gains = jnp.maximum(gains, lax.ppermute(gains, "model", [(i, i ^ 2**n) for i in range(lanes)]))
+        other = lax.ppermute(gains, "model", [(i, i ^ 2**n) for i in range(lanes)])
+        gains = jnp.maximum(gains, other)
+        if n == 2:
+            gains = gains.astype(jnp.bfloat16)
 
     along = {ax: jnp.concatenate([c[OTHER[ax], 1][:unit], c[OTHER[ax], -1][:unit]]) for ax in "xz"}
     e = all_ways(lambda ax, s: along[ax])

time: 144 us -> 139 us (0.965)
  starting transfers between devices: 47.2 us -> 53.1 us
  local copies, waits for them, and re-layouts: 6.31 us -> 1.48 us
  waiting for transfers between devices: 74 us -> 70.2 us
    ppermute x28, starting transfers between devices: 30.9 us -> 35.9 us  [sent(): return lax.ppermute(array, 'fsdp', RING[axis](step))]
    ppermute x6, waiting for transfers between devices: 9.61 us -> 5.77 us  [round_of_max(): others.append(lax.ppermute(values, 'fsdp', ring(step)))]
    unnamed x33 -> x18, local copies, waits for them, and re-layouts: 3.35 us -> 0.05 us
  transfers between devices with their start and end apart: 37 -> 37, of which waited for: 12 -> 11; matrix products, arithmetic and copies ran while one was open for 3% -> 2% of each run, Pallas kernels for 5% -> 5%
where the time goes in v2:
time: 139 us
  waiting for transfers between devices  70.2 us (51%)
  starting transfers between devices  53.1 us (38%)
  Pallas kernels  9.91 us (7%)
  matrix products  2.03 us (1%)
  local copies, waits for them, and re-layouts  1.48 us (1%)
    ppermute x28, waiting for transfers between devices, sent(): return lax.ppermute(array, 'fsdp', RING[axis](step))  64.2 us
    ppermute x28, starting transfers between devices, sent(): return lax.ppermute(array, 'fsdp', RING[axis](step))  35.9 us
    ppermute x6, starting transfers between devices, round_of_max(): others.append(lax.ppermute(values, 'fsdp', ring(step)))  12.4 us
    ppermute x6, waiting for transfers between devices, round_of_max(): others.append(lax.ppermute(values, 'fsdp', ring(step)))  5.77 us
    pallas_call x4, Pallas kernels, placed(): pl.pallas_call(body, out_shape=[jax.ShapeDtypeStruct(f.shape, f.dtype) fo...  5.54 us
    ppermute x3, starting transfers between devices, per_device(): lax.ppermute(gains, 'model', [(i, i ^ 2 ** n) for i in range(lanes)])  4.81 us
  transfers between devices with their start and end apart: 37, of which 11 were waited for; matrix products, arithmetic and copies ran while one was open for 2% of the time, Pallas kernels for 5%

profile of v2, /device:TPU:0, one launch (start us, length us, event | category | flops | bytes accessed | tf_op | source)
XLA Modules:
  0.0 139.1 jit_solution(10980131494846342077)
XLA Ops:
  3.0 4.1 %collective-permute-start = (f32[6400]{0:T(1024)S(1)}, f32[6400]{0:T(1024)S(1)}, u32[]{:S(2)}, u32[]{:S(2)}) collective-permute-start(f32[6400]{0:T(1024)S(1)} %pad_maximum_fusion.6), channel_id=1, source_target_pairs={{0,64},{8,72},{16,80},{24,88},{32,96},{40,104},{48,112},{56,120},{... | collective-permute-start | bytes 76808 | tf_op jit(solution)/shard_map/ppermute | solution.py:286
  8.1 2.2 %collective-permute-start.2 = (f32[6400]{0:T(1024)S(1)}, f32[6400]{0:T(1024)S(1)}, u32[]{:S(2)}, u32[]{:S(2)}) collective-permute-start(f32[6400]{0:T(1024)S(1)} %pad_maximum_fusion.6), channel_id=1, source_target_pairs={{0,96},{8,104},{16,112},{24,120},{32,0},{40,8},{48,16},{56,24},{64... | collective-permute-start | bytes 76808 | tf_op jit(solution)/shard_map/ppermute | solution.py:286
  13.1 1.7 %collective-permute-start.7 = (bf16[160,1408]{1,0:T(8,128)(2,1)S(1)}, bf16[160,1408]{1,0:T(8,128)(2,1)S(1)}, u32[]{:S(2)}, u32[]{:S(2)}) collective-permute-start(bf16[160,1408]{1,0:T(8,128)(2,1)S(1)} %get-tuple-element.35.refs_6_), channel_id=1, source_target_pairs={{0,24},{8,0},{16,8},{24,16},{32,56},{40,32},{48,40},{56,48},{64,88... | collective-permute-start | bytes 1351688 | tf_op jit(solution)/shard_map/ppermute | solution.py:36
  15.0 1.9 %collective-permute-start.3 = (f32[6400]{0:T(1024)S(1)}, f32[6400]{0:T(1024)S(1)}, u32[]{:S(2)}, u32[]{:S(2)}) collective-permute-start(f32[6400]{0:T(1024)S(1)} %maximum_maximum_fusion.1), channel_id=1, source_target_pairs={{0,16},{8,24},{16,0},{24,8},{32,48},{40,56},{48,32},{56,40},{64,80... | collective-permute-start | bytes 76808 | tf_op jit(solution)/shard_map/ppermute | solution.py:286
  17.5 2.6 %collective-permute-start.5 = (f32[6400]{0:T(1024)S(1)}, f32[6400]{0:T(1024)S(1)}, u32[]{:S(2)}, u32[]{:S(2)}) collective-permute-start(f32[6400]{0:T(1024)S(1)} %maximum_maximum_fusion.1), channel_id=1, source_target_pairs={{0,24},{8,0},{16,8},{24,16},{32,56},{40,32},{48,40},{56,48},{64,88... | collective-permute-start | bytes 76808 | tf_op jit(solution)/shard_map/ppermute | solution.py:286
  20.2 5.8 %collective-permute-done.3 = f32[6400]{0:T(1024)S(1)} collective-permute-done((f32[6400]{0:T(1024)S(1)}, f32[6400]{0:T(1024)S(1)}, u32[]{:S(2)}, u32[]{:S(2)}) %collective-permute-start.3) | collective-permute-done | bytes 25632 | tf_op jit(solution)/shard_map/ppermute | solution.py:286
  26.0 3.2 %collective-permute-start.9 = (bf16[160,1408]{1,0:T(8,128)(2,1)S(1)}, bf16[160,1408]{1,0:T(8,128)(2,1)S(1)}, u32[]{:S(2)}, u32[]{:S(2)}) collective-permute-start(bf16[160,1408]{1,0:T(8,128)(2,1)S(1)} %get-tuple-element.36.refs_7_), channel_id=1, source_target_pairs={{0,96},{8,104},{16,112},{24,120},{32,0},{40,8},{48,16},{56,24},{64... | collective-permute-start | bytes 1351688 | tf_op jit(solution)/shard_map/ppermute | solution.py:36
  29.3 7.7 %collective-permute-done.8.refs_4_ = bf16[160,1408]{1,0:T(8,128)(2,1)S(1)} collective-permute-done((bf16[160,1408]{1,0:T(8,128)(2,1)S(1)}, bf16[160,1408]{1,0:T(8,128)(2,1)S(1)}, u32[]{:S(2)}, u32[]{:S(2)}) %collective-permute-start.8) | collective-permute-done | bytes 450592 | tf_op jit(solution)/shard_map/ppermute | solution.py:36
  43.3 2.6 %collective-permute-start.27 = (bf16[160,1408]{1,0:T(8,128)(2,1)S(1)}, bf16[160,1408]{1,0:T(8,128)(2,1)S(1)}, u32[]{:S(2)}, u32[]{:S(2)}) collective-permute-start(bf16[160,1408]{1,0:T(8,128)(2,1)S(1)} %get-tuple-element.36.refs_7_), channel_id=1, source_target_pairs={{0,24},{8,0},{16,8},{24,16},{32,56},{40,32},{48,40},{56,48},{64,88... | collective-permute-start | bytes 1351688 | tf_op jit(solution)/shard_map/ppermute | solution.py:36
  46.0 8.2 %collective-permute-done.26.refs_2_ = bf16[160,1408]{1,0:T(8,128)(2,1)S(1)} collective-permute-done((bf16[160,1408]{1,0:T(8,128)(2,1)S(1)}, bf16[160,1408]{1,0:T(8,128)(2,1)S(1)}, u32[]{:S(2)}, u32[]{:S(2)}) %collective-permute-start.26) | collective-permute-done | bytes 450592 | tf_op jit(solution)/shard_map/ppermute | solution.py:36
  54.2 3.0 %collective-permute-start.29 = (bf16[160,1408]{1,0:T(8,128)(2,1)S(1)}, bf16[160,1408]{1,0:T(8,128)(2,1)S(1)}, u32[]{:S(2)}, u32[]{:S(2)}) collective-permute-start(bf16[160,1408]{1,0:T(8,128)(2,1)S(1)} %get-tuple-element.35.refs_6_), channel_id=1, source_target_pairs={{0,96},{8,104},{16,112},{24,120},{32,0},{40,8},{48,16},{56,24},{64... | collective-permute-start | bytes 1351688 | tf_op jit(solution)/shard_map/ppermute | solution.py:36
  57.1 12.2 %collective-permute-done.27.refs_3_ = bf16[160,1408]{1,0:T(8,128)(2,1)S(1)} collective-permute-done((bf16[160,1408]{1,0:T(8,128)(2,1)S(1)}, bf16[160,1408]{1,0:T(8,128)(2,1)S(1)}, u32[]{:S(2)}, u32[]{:S(2)}) %collective-permute-start.27) | collective-permute-done | bytes 450592 | tf_op jit(solution)/shard_map/ppermute | solution.py:36
  69.4 3.2 %collective-permute-start.36 = (bf16[5120]{0:T(1024)(128)(2,1)S(1)}, bf16[5120]{0:T(1024)(128)(2,1)S(1)}, u32[]{:S(2)}, u32[]{:S(2)}) collective-permute-start(bf16[5120]{0:T(1024)(128)(2,1)S(1)} %max.34), channel_id=1, source_target_pairs={{0,4},{1,5},{2,6},{3,7},{4,0},{5,1},{6,2},{7,3},{8,12},{9,13},{10,... | collective-permute-start | bytes 30728 | tf_op jit(solution)/shard_map/ppermute | solution.py:349
  74.9 2.7 %collective-permute-start.31 = (bf16[80,1280]{1,0:T(8,128)(2,1)S(1)}, bf16[80,1280]{1,0:T(8,128)(2,1)S(1)}, u32[]{:S(2)}, u32[]{:S(2)}) collective-permute-start(bf16[80,1280]{1,0:T(8,128)(2,1)S(1)} %get-tuple-element.45), channel_id=1, source_target_pairs={{0,24},{8,0},{16,8},{24,16},{32,56},{40,32},{48,40},{56,48},{64,88... | collective-permute-start | bytes 614408 | tf_op jit(solution)/shard_map/ppermute | solution.py:36
  77.6 2.7 %collective-permute-start.11 = (bf16[400,1280]{1,0:T(8,128)(2,1)S(1)}, bf16[400,1280]{1,0:T(8,128)(2,1)S(1)}, u32[]{:S(2)}, u32[]{:S(2)}) collective-permute-start(bf16[400,1280]{1,0:T(8,128)(2,1)S(1)} %get-tuple-element.38), channel_id=1, source_target_pairs={{0,96},{8,104},{16,112},{24,120},{32,0},{40,8},{48,16},{56,24},{64... | collective-permute-start | bytes 3072008 | tf_op jit(solution)/shard_map/ppermute | solution.py:36
  80.5 18.7 %collective-permute-done.11.refs_3_ = bf16[400,1280]{1,0:T(8,128)(2,1)S(1)} collective-permute-done((bf16[400,1280]{1,0:T(8,128)(2,1)S(1)}, bf16[400,1280]{1,0:T(8,128)(2,1)S(1)}, u32[]{:S(2)}, u32[]{:S(2)}) %collective-permute-start.11) | collective-permute-done | bytes 1024032 | tf_op jit(solution)/shard_map/ppermute | solution.py:36
  99.3 6.4 %collective-permute-done.10.refs_2_ = bf16[400,1280]{1,0:T(8,128)(2,1)S(1)} collective-permute-done((bf16[400,1280]{1,0:T(8,128)(2,1)S(1)}, bf16[400,1280]{1,0:T(8,128)(2,1)S(1)}, u32[]{:S(2)}, u32[]{:S(2)}) %collective-permute-start.10) | collective-permute-done | bytes 1024032 | tf_op jit(solution)/shard_map/ppermute | solution.py:36
  106.1 2.1 %collective-permute-start.32 = (bf16[80,1280]{1,0:T(8,128)(2,1)S(1)}, bf16[80,1280]{1,0:T(8,128)(2,1)S(1)}, u32[]{:S(2)}, u32[]{:S(2)}) collective-permute-start(bf16[80,1280]{1,0:T(8,128)(2,1)S(1)} %get-tuple-element.46), channel_id=1, source_target_pairs={{0,32},{8,40},{16,48},{24,56},{32,64},{40,72},{48,80},{56,88},{64,... | collective-permute-start | bytes 614408 | tf_op jit(solution)/shard_map/ppermute | solution.py:36
  108.2 3.2 %collective-permute-start.14 = (bf16[160,1280]{1,0:T(8,128)(2,1)S(1)}, bf16[160,1280]{1,0:T(8,128)(2,1)S(1)}, u32[]{:S(2)}, u32[]{:S(2)}) collective-permute-start(bf16[160,1280]{1,0:T(8,128)(2,1)S(1)} %pad_maximum_fusion), channel_id=1, source_target_pairs={{0,24},{8,0},{16,8},{24,16},{32,56},{40,32},{48,40},{56,48},{64,88... | collective-permute-start | bytes 1228808 | tf_op jit(solution)/shard_map/ppermute | solution.py:36
  111.4 3.4 %collective-permute-done.32.refs_2_ = bf16[80,1280]{1,0:T(8,128)(2,1)S(1)} collective-permute-done((bf16[80,1280]{1,0:T(8,128)(2,1)S(1)}, bf16[80,1280]{1,0:T(8,128)(2,1)S(1)}, u32[]{:S(2)}, u32[]{:S(2)}) %collective-permute-start.32) | collective-permute-done | bytes 204832 | tf_op jit(solution)/shard_map/ppermute | solution.py:36
  117.0 3.7 %collective-permute-start.23 = (bf16[160,1280]{1,0:T(8,128)(2,1)S(1)}, bf16[160,1280]{1,0:T(8,128)(2,1)S(1)}, u32[]{:S(2)}, u32[]{:S(2)}) collective-permute-start(bf16[160,1280]{1,0:T(8,128)(2,1)S(1)} %pad_maximum_fusion.3), channel_id=1, source_target_pairs={{0,24},{8,0},{16,8},{24,16},{32,56},{40,32},{48,40},{56,48},{64,88... | collective-permute-start | bytes 1228808 | tf_op jit(solution)/shard_map/ppermute | solution.py:36
  123.5 5.4 %collective-permute-done.25.refs_7_ = bf16[160,1280]{1,0:T(8,128)(2,1)S(1)} collective-permute-done((bf16[160,1280]{1,0:T(8,128)(2,1)S(1)}, bf16[160,1280]{1,0:T(8,128)(2,1)S(1)}, u32[]{:S(2)}, u32[]{:S(2)}) %collective-permute-start.25) | collective-permute-done | bytes 409632 | tf_op jit(solution)/shard_map/ppermute | solution.py:36
  129.6 2.6 %collective-permute-start.15 = (bf16[80,1280]{1,0:T(8,128)(2,1)S(1)}, bf16[80,1280]{1,0:T(8,128)(2,1)S(1)}, u32[]{:S(2)}, u32[]{:S(2)}) collective-permute-start(bf16[80,1280]{1,0:T(8,128)(2,1)S(1)} %slice.88), channel_id=1, source_target_pairs={{0,24},{8,0},{16,8},{24,16},{32,56},{40,32},{48,40},{56,48},{64,88... | collective-permute-start | bytes 614408 | tf_op jit(solution)/shard_map/ppermute | solution.py:36
  134.2 2.0 %shard_map.163 = (bf16[5120,1024]{1,0:T(8,128)(2,1)}, bf16[5120,128]{1,0:T(8,128)(2,1)}, bf16[5120,128]{1,0:T(8,128)(2,1)}) custom-call(bf16[400,1280]{1,0:T(8,128)(2,1)S(1)} %collective-permute-done.16.refs_0_, bf16[400,1280]{1,0:T(8,128)(2,1)S(1)} %collective-permute-done.17.refs_1_, ...), custom_call_target="tpu_custom_call", output_to_operand_aliasing={{0}: (4, {}), {1}: (5, {}), {2}: (6, {})} | custom-call | tf_op jit(solution)/shard_map/pallas_call | solution.py:224
  (110 shorter events, 26.5 us)
Async XLA Ops:
  3.0 11.9 %collective-permute-start = (f32[6400]{0:T(1024)S(1)}, f32[6400]{0:T(1024)S(1)}, u32[]{:S(2)}, u32[]{:S(2)}) collective-permute-start(f32[6400]{0:T(1024)S(1)} %pad_maximum_fusion.6), channel_id=1, source_target_pairs={{0,64},{8,72},{16,80},{24,88},{32,96},{40,104},{48,112},{56,120},{... | collective-permute-start | bytes 76808 | tf_op jit(solution)/shard_map/ppermute | solution.py:286
  11.5 17.7 %collective-permute-start.6 = (bf16[160,1408]{1,0:T(8,128)(2,1)S(1)}, bf16[160,1408]{1,0:T(8,128)(2,1)S(1)}, u32[]{:S(2)}, u32[]{:S(2)}) collective-permute-start(bf16[160,1408]{1,0:T(8,128)(2,1)S(1)} %get-tuple-element.35.refs_6_), channel_id=1, source_target_pairs={{0,8},{8,16},{16,24},{24,0},{32,40},{40,48},{48,56},{56,32},{64,72... | collective-permute-start | bytes 1351688 | tf_op jit(solution)/shard_map/ppermute | solution.py:36
  13.1 16.2 %collective-permute-start.7 = (bf16[160,1408]{1,0:T(8,128)(2,1)S(1)}, bf16[160,1408]{1,0:T(8,128)(2,1)S(1)}, u32[]{:S(2)}, u32[]{:S(2)}) collective-permute-start(bf16[160,1408]{1,0:T(8,128)(2,1)S(1)} %get-tuple-element.35.refs_6_), channel_id=1, source_target_pairs={{0,24},{8,0},{16,8},{24,16},{32,56},{40,32},{48,40},{56,48},{64,88... | collective-permute-start | bytes 1351688 | tf_op jit(solution)/shard_map/ppermute | solution.py:36
  17.5 11.7 %collective-permute-start.5 = (f32[6400]{0:T(1024)S(1)}, f32[6400]{0:T(1024)S(1)}, u32[]{:S(2)}, u32[]{:S(2)}) collective-permute-start(f32[6400]{0:T(1024)S(1)} %maximum_maximum_fusion.1), channel_id=1, source_target_pairs={{0,24},{8,0},{16,8},{24,16},{32,56},{40,32},{48,40},{56,48},{64,88... | collective-permute-start | bytes 76808 | tf_op jit(solution)/shard_map/ppermute | solution.py:286
  26.0 11.0 %collective-permute-start.8 = (bf16[160,1408]{1,0:T(8,128)(2,1)S(1)}, bf16[160,1408]{1,0:T(8,128)(2,1)S(1)}, u32[]{:S(2)}, u32[]{:S(2)}) collective-permute-start(bf16[160,1408]{1,0:T(8,128)(2,1)S(1)} %get-tuple-element.36.refs_7_), channel_id=1, source_target_pairs={{0,32},{8,40},{16,48},{24,56},{32,64},{40,72},{48,80},{56,88},{64,... | collective-permute-start | bytes 1351688 | tf_op jit(solution)/shard_map/ppermute | solution.py:36
  38.4 39.1 %collective-permute-start.17 = (bf16[400,1280]{1,0:T(8,128)(2,1)S(1)}, bf16[400,1280]{1,0:T(8,128)(2,1)S(1)}, u32[]{:S(2)}, u32[]{:S(2)}) collective-permute-start(bf16[400,1280]{1,0:T(8,128)(2,1)S(1)} %get-tuple-element.40), channel_id=1, source_target_pairs={{0,24},{8,0},{16,8},{24,16},{32,56},{40,32},{48,40},{56,48},{64,88... | collective-permute-start | bytes 3072008 | tf_op jit(solution)/shard_map/ppermute | solution.py:36
  39.9 14.3 %collective-permute-start.26 = (bf16[160,1408]{1,0:T(8,128)(2,1)S(1)}, bf16[160,1408]{1,0:T(8,128)(2,1)S(1)}, u32[]{:S(2)}, u32[]{:S(2)}) collective-permute-start(bf16[160,1408]{1,0:T(8,128)(2,1)S(1)} %get-tuple-element.36.refs_7_), channel_id=1, source_target_pairs={{0,8},{8,16},{16,24},{24,0},{32,40},{40,48},{48,56},{56,32},{64,72... | collective-permute-start | bytes 1351688 | tf_op jit(solution)/shard_map/ppermute | solution.py:36
  40.5 39.8 %collective-permute-start.16 = (bf16[400,1280]{1,0:T(8,128)(2,1)S(1)}, bf16[400,1280]{1,0:T(8,128)(2,1)S(1)}, u32[]{:S(2)}, u32[]{:S(2)}) collective-permute-start(bf16[400,1280]{1,0:T(8,128)(2,1)S(1)} %get-tuple-element.39), channel_id=1, source_target_pairs={{0,8},{8,16},{16,24},{24,0},{32,40},{40,48},{48,56},{56,32},{64,72... | collective-permute-start | bytes 3072008 | tf_op jit(solution)/shard_map/ppermute | solution.py:36
  43.3 26.0 %collective-permute-start.27 = (bf16[160,1408]{1,0:T(8,128)(2,1)S(1)}, bf16[160,1408]{1,0:T(8,128)(2,1)S(1)}, u32[]{:S(2)}, u32[]{:S(2)}) collective-permute-start(bf16[160,1408]{1,0:T(8,128)(2,1)S(1)} %get-tuple-element.36.refs_7_), channel_id=1, source_target_pairs={{0,24},{8,0},{16,8},{24,16},{32,56},{40,32},{48,40},{56,48},{64,88... | collective-permute-start | bytes 1351688 | tf_op jit(solution)/shard_map/ppermute | solution.py:36
  46.0 26.5 %collective-permute-start.28 = (bf16[160,1408]{1,0:T(8,128)(2,1)S(1)}, bf16[160,1408]{1,0:T(8,128)(2,1)S(1)}, u32[]{:S(2)}, u32[]{:S(2)}) collective-permute-start(bf16[160,1408]{1,0:T(8,128)(2,1)S(1)} %get-tuple-element.35.refs_6_), channel_id=1, source_target_pairs={{0,32},{8,40},{16,48},{24,56},{32,64},{40,72},{48,80},{56,88},{64,... | collective-permute-start | bytes 1351688 | tf_op jit(solution)/shard_map/ppermute | solution.py:36
  54.2 18.4 %collective-permute-start.29 = (bf16[160,1408]{1,0:T(8,128)(2,1)S(1)}, bf16[160,1408]{1,0:T(8,128)(2,1)S(1)}, u32[]{:S(2)}, u32[]{:S(2)}) collective-permute-start(bf16[160,1408]{1,0:T(8,128)(2,1)S(1)} %get-tuple-element.35.refs_6_), channel_id=1, source_target_pairs={{0,96},{8,104},{16,112},{24,120},{32,0},{40,8},{48,16},{56,24},{64... | collective-permute-start | bytes 1351688 | tf_op jit(solution)/shard_map/ppermute | solution.py:36
  69.4 36.4 %collective-permute-start.36 = (bf16[5120]{0:T(1024)(128)(2,1)S(1)}, bf16[5120]{0:T(1024)(128)(2,1)S(1)}, u32[]{:S(2)}, u32[]{:S(2)}) collective-permute-start(bf16[5120]{0:T(1024)(128)(2,1)S(1)} %max.34), channel_id=1, source_target_pairs={{0,4},{1,5},{2,6},{3,7},{4,0},{5,1},{6,2},{7,3},{8,12},{9,13},{10,... | collective-permute-start | bytes 30728 | tf_op jit(solution)/shard_map/ppermute | solution.py:349
  74.3 31.8 %collective-permute-start.30 = (bf16[80,1280]{1,0:T(8,128)(2,1)S(1)}, bf16[80,1280]{1,0:T(8,128)(2,1)S(1)}, u32[]{:S(2)}, u32[]{:S(2)}) collective-permute-start(bf16[80,1280]{1,0:T(8,128)(2,1)S(1)} %get-tuple-element.44), channel_id=1, source_target_pairs={{0,8},{8,16},{16,24},{24,0},{32,40},{40,48},{48,56},{56,32},{64,72... | collective-permute-start | bytes 614408 | tf_op jit(solution)/shard_map/ppermute | solution.py:36
  74.9 33.3 %collective-permute-start.31 = (bf16[80,1280]{1,0:T(8,128)(2,1)S(1)}, bf16[80,1280]{1,0:T(8,128)(2,1)S(1)}, u32[]{:S(2)}, u32[]{:S(2)}) collective-permute-start(bf16[80,1280]{1,0:T(8,128)(2,1)S(1)} %get-tuple-element.45), channel_id=1, source_target_pairs={{0,24},{8,0},{16,8},{24,16},{32,56},{40,32},{48,40},{56,48},{64,88... | collective-permute-start | bytes 614408 | tf_op jit(solution)/shard_map/ppermute | solution.py:36
  77.6 21.6 %collective-permute-start.11 = (bf16[400,1280]{1,0:T(8,128)(2,1)S(1)}, bf16[400,1280]{1,0:T(8,128)(2,1)S(1)}, u32[]{:S(2)}, u32[]{:S(2)}) collective-permute-start(bf16[400,1280]{1,0:T(8,128)(2,1)S(1)} %get-tuple-element.38), channel_id=1, source_target_pairs={{0,96},{8,104},{16,112},{24,120},{32,0},{40,8},{48,16},{56,24},{64... | collective-permute-start | bytes 3072008 | tf_op jit(solution)/shard_map/ppermute | solution.py:36
  80.3 25.4 %collective-permute-start.10 = (bf16[400,1280]{1,0:T(8,128)(2,1)S(1)}, bf16[400,1280]{1,0:T(8,128)(2,1)S(1)}, u32[]{:S(2)}, u32[]{:S(2)}) collective-permute-start(bf16[400,1280]{1,0:T(8,128)(2,1)S(1)} %get-tuple-element.37), channel_id=1, source_target_pairs={{0,32},{8,40},{16,48},{24,56},{32,64},{40,72},{48,80},{56,88},{64,... | collective-permute-start | bytes 3072008 | tf_op jit(solution)/shard_map/ppermute | solution.py:36
  99.2 15.7 %collective-permute-start.18 = (bf16[160,1280]{1,0:T(8,128)(2,1)S(1)}, bf16[160,1280]{1,0:T(8,128)(2,1)S(1)}, u32[]{:S(2)}, u32[]{:S(2)}) collective-permute-start(bf16[160,1280]{1,0:T(8,128)(2,1)S(1)} %pad_maximum_fusion.1), channel_id=1, source_target_pairs={{0,32},{8,40},{16,48},{24,56},{32,64},{40,72},{48,80},{56,88},{64,... | collective-permute-start | bytes 1228808 | tf_op jit(solution)/shard_map/ppermute | solution.py:36
  105.8 11.2 %collective-permute-start.12 = (bf16[160,1280]{1,0:T(8,128)(2,1)S(1)}, bf16[160,1280]{1,0:T(8,128)(2,1)S(1)}, u32[]{:S(2)}, u32[]{:S(2)}) collective-permute-start(bf16[160,1280]{1,0:T(8,128)(2,1)S(1)} %pad_maximum_fusion), channel_id=1, source_target_pairs={{0,8},{8,16},{16,24},{24,0},{32,40},{40,48},{48,56},{56,32},{64,72... | collective-permute-start | bytes 1228808 | tf_op jit(solution)/shard_map/ppermute | solution.py:36
  108.2 12.5 %collective-permute-start.14 = (bf16[160,1280]{1,0:T(8,128)(2,1)S(1)}, bf16[160,1280]{1,0:T(8,128)(2,1)S(1)}, u32[]{:S(2)}, u32[]{:S(2)}) collective-permute-start(bf16[160,1280]{1,0:T(8,128)(2,1)S(1)} %pad_maximum_fusion), channel_id=1, source_target_pairs={{0,24},{8,0},{16,8},{24,16},{32,56},{40,32},{48,40},{56,48},{64,88... | collective-permute-start | bytes 1228808 | tf_op jit(solution)/shard_map/ppermute | solution.py:36
  114.8 14.0 %collective-permute-start.25 = (bf16[160,1280]{1,0:T(8,128)(2,1)S(1)}, bf16[160,1280]{1,0:T(8,128)(2,1)S(1)}, u32[]{:S(2)}, u32[]{:S(2)}) collective-permute-start(bf16[160,1280]{1,0:T(8,128)(2,1)S(1)} %pad_maximum_fusion.5), channel_id=1, source_target_pairs={{0,96},{8,104},{16,112},{24,120},{32,0},{40,8},{48,16},{56,24},{64... | collective-permute-start | bytes 1228808 | tf_op jit(solution)/shard_map/ppermute | solution.py:36
  116.0 12.9 %collective-permute-start.24 = (bf16[160,1280]{1,0:T(8,128)(2,1)S(1)}, bf16[160,1280]{1,0:T(8,128)(2,1)S(1)}, u32[]{:S(2)}, u32[]{:S(2)}) collective-permute-start(bf16[160,1280]{1,0:T(8,128)(2,1)S(1)} %pad_maximum_fusion.4), channel_id=1, source_target_pairs={{0,32},{8,40},{16,48},{24,56},{32,64},{40,72},{48,80},{56,88},{64,... | collective-permute-start | bytes 1228808 | tf_op jit(solution)/shard_map/ppermute | solution.py:36
  117.0 12.6 %collective-permute-start.23 = (bf16[160,1280]{1,0:T(8,128)(2,1)S(1)}, bf16[160,1280]{1,0:T(8,128)(2,1)S(1)}, u32[]{:S(2)}, u32[]{:S(2)}) collective-permute-start(bf16[160,1280]{1,0:T(8,128)(2,1)S(1)} %pad_maximum_fusion.3), channel_id=1, source_target_pairs={{0,24},{8,0},{16,8},{24,16},{32,56},{40,32},{48,40},{56,48},{64,88... | collective-permute-start | bytes 1228808 | tf_op jit(solution)/shard_map/ppermute | solution.py:36
  120.7 15.5 %collective-permute-start.22 = (bf16[160,1280]{1,0:T(8,128)(2,1)S(1)}, bf16[160,1280]{1,0:T(8,128)(2,1)S(1)}, u32[]{:S(2)}, u32[]{:S(2)}) collective-permute-start(bf16[160,1280]{1,0:T(8,128)(2,1)S(1)} %pad_maximum_fusion.2), channel_id=1, source_target_pairs={{0,8},{8,16},{16,24},{24,0},{32,40},{40,48},{48,56},{56,32},{64,72... | collective-permute-start | bytes 1228808 | tf_op jit(solution)/shard_map/ppermute | solution.py:36
  122.4 15.5 %collective-permute-start.19 = (bf16[80,1280]{1,0:T(8,128)(2,1)S(1)}, bf16[80,1280]{1,0:T(8,128)(2,1)S(1)}, u32[]{:S(2)}, u32[]{:S(2)}) collective-permute-start(bf16[80,1280]{1,0:T(8,128)(2,1)S(1)} %slice.91), channel_id=1, source_target_pairs={{0,32},{8,40},{16,48},{24,56},{32,64},{40,72},{48,80},{56,88},{64,... | collective-permute-start | bytes 614408 | tf_op jit(solution)/shard_map/ppermute | solution.py:36
  (22 other events, 133.8 us)

commit v3 on v2

--- a/solution.py
+++ b/solution.py
@@ -232,17 +232,29 @@
     )(*[in_vmem(array) for array in arrays], *finals)
 
 
-def packed(weights, lows, widths):
+def doubled_max(values):
+    for bit in (SIDE, 3 * SIDE, 1, 3):
+        other = lax.ppermute(values, "fsdp", [(i, i ^ bit) for i in range(SIDE * SIDE)])
+        values = jnp.maximum(values, other)
+    return values
+
+
+def packed(weights, lows, highs, norms, widths):
     rows, wide = weights[0].shape[0], sum(widths)
     half, rank, count = rows // 2, lows[0].shape[1], len(weights)
+    tile, deep = 2 * LANES, LANES // 2
+    cell = norms[0].shape
 
     def body(*refs):
-        sources, turned, outs = refs[:count], refs[count : 2 * count], refs[2 * count : 2 * count + 2]
-        stage, sems = refs[-2], refs[-1]
-        low_copies = [
-            pltpu.make_async_copy(turned[n], stage.at[n], sems.at[n])
-            for n in range(count)
+        sources, turned, factors = refs[:count], refs[count : 2 * count], refs[2 * count : 3 * count]
+        outs, largest, spreads = refs[3 * count + 2 : 3 * count + 4], refs[3 * count + 4], refs[3 * count + 5 : 3 * count + 7]
+        gain, stage, held, sems = refs[-4:]
+        norm_copies = [
+            pltpu.make_async_copy(refs[3 * count + n], held.at[n], sems.at[4 * count + n]) for n in (0, 1)
         ]
+        for copy in norm_copies:
+            copy.start()
+        low_copies = [pltpu.make_async_copy(turned[n], stage.at[n], sems.at[n]) for n in range(count)]
         for copy in low_copies:
             copy.start()
         copies, at = [], 0
@@ -257,6 +269,19 @@
                 )
                 copies[-1].start()
             at += width
+        for part in spreads:
+            part[...] = jnp.zeros(part.shape, part.dtype)
+        at = 0
+        for n, width in enumerate(widths):
+            copies.append(
+                pltpu.make_async_copy(
+                    factors[n],
+                    spreads[n * rank // deep].at[pl.ds(n * rank % deep, rank), pl.ds(at, width)],
+                    sems.at[3 * count + n],
+                )
+            )
+            copies[-1].start()
+            at += width
         for copy in low_copies:
             copy.wait()
         low = jnp.concatenate(
@@ -268,23 +293,36 @@
             outs[h][:, wide:] = straight[h * half : (h + 1) * half]
         for copy in copies:
             copy.wait()
-
+        for t in range(0, wide, tile):
+            best = None
+            factor = jnp.concatenate([part[:, t : t + tile] for part in spreads])
+            for h in (0, 1):
+                update = jnp.dot(outs[h][:, wide:], factor, preferred_element_type=jnp.float32)
+                value = jnp.abs(outs[h][:, t : t + tile].astype(jnp.float32) + mix_rate * update)
+                value = jnp.max(value, axis=0, keepdims=True)
+                best = value if best is None else jnp.maximum(best, value)
+            largest[:, t : t + tile] = best
+        for copy in norm_copies:
+            copy.wait()
+        gain[...] = (held[0] + held[1]).astype(jnp.bfloat16).astype(jnp.float32)
+
+    hbm = pltpu.MemorySpace.HBM
     return pl.pallas_call(
         body,
-        out_shape=[jax.ShapeDtypeStruct((half, wide + LANES), jnp.bfloat16)] * 2,
-        in_specs=[pl.BlockSpec(memory_space=pltpu.MemorySpace.HBM)] * (2 * count),
-        out_specs=[VMEM] * 2,
-        scratch_shapes=[pltpu.VMEM((count, rank, rows), jnp.bfloat16), pltpu.SemaphoreType.DMA((3 * count,))],
+        out_shape=[jax.ShapeDtypeStruct((half, wide + LANES), jnp.bfloat16)] * 2
+        + [jax.ShapeDtypeStruct((1, wide), jnp.float32)]
+        + [jax.ShapeDtypeStruct((deep, wide), jnp.bfloat16)] * 2
+        + [jax.ShapeDtypeStruct(cell, jnp.float32)],
+        in_specs=[pl.BlockSpec(memory_space=hbm)] * (3 * count + 2),
+        out_specs=[VMEM] * 6,
+        scratch_shapes=[
+            pltpu.VMEM((count, rank, rows), jnp.bfloat16),
+            pltpu.VMEM((2, *cell), jnp.float32),
+            pltpu.SemaphoreType.DMA((4 * count + 2,)),
+        ],
         compiler_params=pltpu.CompilerParams(vmem_limit_bytes=4 * 2**20),
         name="packed",
-    )(*[pltpu.with_memory_space_constraint(a, pltpu.MemorySpace.HBM) for a in (*weights, *[low.T for low in lows])])
-
-
-def round_of_max(values, ring):
-    others = []
-    for step in (2, 1, -1):
-        others.append(lax.ppermute(values, "fsdp", ring(step)))
-    return jnp.maximum(jnp.maximum(values, others[0]), jnp.maximum(others[1], others[2]))
+    )(*[pltpu.with_memory_space_constraint(a, hbm) for a in (*weights, *[low.T for low in lows], *highs, *norms)])
 
 
 def per_device(
@@ -307,37 +345,28 @@
     lows = (low_query, low_key, low_value)
     highs = (high_query, high_key, high_value)
     widths = [w.shape[1] for w in weights]
-    wide, ranks = sum(widths), [low.shape[1] for low in lows]
+    wide = sum(widths)
     rows = weight_query.shape[0]
     unit = rows // 4
-    rest = LANES - sum(ranks)
-    norm = (norm_train + norm_step).astype(jnp.bfloat16).astype(jnp.float32)
+    *halves, largest, spread_0, spread_1, norm = packed(
+        weights, lows, highs, [n.reshape(1, -1) for n in (norm_train, norm_step)], widths
+    )
+    size = norm.shape[1]
     slots = lax.dynamic_update_slice(
-        jnp.full((groups * lanes * norm.shape[0],), -jnp.inf), norm, ((me * lanes + lane) * norm.shape[0],)
+        jnp.full((groups * lanes * size,), -jnp.inf), norm.reshape(-1), ((me * lanes + lane) * size,)
     )
-    halves = packed(weights, lows, widths)
     a = all_ways(lambda ax, s: halves[LEAD[ax]])
     b = all_ways(lambda ax, s: halves[1 - LEAD[ax]])
 
-    largest = [
-        jnp.max(
-            jnp.abs(w.astype(jnp.float32) + mix_rate * jnp.dot(low, high, preferred_element_type=jnp.float32)),
-            axis=0,
-        )
-        for w, low, high in zip(weights, lows, highs)
-    ]
-    shared = round_of_max(jnp.concatenate([*largest, slots]), z_ring)
-    shared = round_of_max(shared, x_ring)
+    shared = doubled_max(jnp.concatenate([largest.reshape(-1), slots]))
     columns, at = [], 0
     for width in widths:
         columns.append(shared[at : at + width])
         at += width
     inverse = (1.0 / shared[:wide]).reshape(1, wide)
-    mixed, at = [], 0
-    for high, width in zip(highs, widths):
-        mixed.append(jnp.pad(mix_rate * high, ((0, 0), (at, wide - at - width))))
-        at += width
-    mixed = jnp.concatenate([*mixed, jnp.zeros((rest, wide), jnp.bfloat16)], axis=0)
+    scaled_0 = mix_rate * spread_0
+    scaled_1 = mix_rate * spread_1
+    mixed = jnp.concatenate([scaled_0, scaled_1])
 
     messages, finals = first_hop(a, unit, mixed, inverse, widths)
     c = all_ways(lambda ax, s: messages[ax, s])
@@ -346,7 +375,7 @@
 
     gains = shared[wide:]
     for n in range(3):
-        other = lax.ppermute(gains, "model", [(i, i ^ 2**n) for i in range(lanes)])
+        other = lax.ppermute(gains, "model", [(i, i ^ (1, 2, 6)[n]) for i in range(lanes)])
         gains = jnp.maximum(gains, other)
         if n == 2:
             gains = gains.astype(jnp.bfloat16)

time: 139 us -> 128 us (0.921)
  starting transfers between devices: 53.1 us -> 43.2 us
  matrix products: 2.03 us -> 0 us
    ppermute x9 -> x7, waiting for transfers between devices: 6.01 us -> 12 us  [the longest x4 11 us: doubled_max(): lax.ppermute(values, 'fsdp', [(i, i ^ bit) for i in range(SIDE * SIDE)])]
    ppermute x28, waiting for transfers between devices: 64.2 us -> 58.5 us  [sent(): return lax.ppermute(array, 'fsdp', RING[axis](step))]
    ppermute x28, starting transfers between devices: 35.9 us -> 30.3 us  [sent(): return lax.ppermute(array, 'fsdp', RING[axis](step))]
    ppermute x9 -> x7, starting transfers between devices: 17.2 us -> 12.9 us  [the longest x4 8.23 us: doubled_max(): lax.ppermute(values, 'fsdp', [(i, i ^ bit) for i in range(SIDE * SIDE)])]
    dot_general x3 -> x0, matrix products: 2.03 us -> none  [per_device(): jnp.dot(low, high, preferred_element_type=jnp.float32)]
  transfers between devices with their start and end apart: 37 -> 35, of which waited for: 11 -> 12; matrix products, arithmetic and copies ran while one was open for 2% -> 2% of each run, Pallas kernels for 5% -> 5%
where the time goes in v3:
time: 128 us
  waiting for transfers between devices  70.4 us (55%)
  starting transfers between devices  43.2 us (34%)
  Pallas kernels  10.4 us (8%)
  local copies, waits for them, and re-layouts  1.47 us (1%)
    ppermute x28, waiting for transfers between devices, sent(): return lax.ppermute(array, 'fsdp', RING[axis](step))  58.5 us
    ppermute x28, starting transfers between devices, sent(): return lax.ppermute(array, 'fsdp', RING[axis](step))  30.3 us
    ppermute x4, waiting for transfers between devices, doubled_max(): lax.ppermute(values, 'fsdp', [(i, i ^ bit) for i in range(SIDE * SIDE)])  11 us
    ppermute x4, starting transfers between devices, doubled_max(): lax.ppermute(values, 'fsdp', [(i, i ^ bit) for i in range(SIDE * SIDE)])  8.23 us
    pallas_call x4, Pallas kernels, placed(): pl.pallas_call(body, out_shape=[jax.ShapeDtypeStruct(f.shape, f.dtype) fo...  5.54 us
    ppermute x3, starting transfers between devices, per_device(): lax.ppermute(gains, 'model', [(i, i ^ (1, 2, 6)[n]) for i in range(lanes)])  4.68 us
  transfers between devices with their start and end apart: 35, of which 12 were waited for; matrix products, arithmetic and copies ran while one was open for 2% of the time, Pallas kernels for 5%

profile of v3, /device:TPU:0, one launch (start us, length us, event | category | flops | bytes accessed | tf_op | source)
XLA Modules:
  0.0 127.5 jit_solution(8629351051004167377)
XLA Ops:
  2.5 2.1 %collective-permute-start = (f32[6400]{0:T(1024)S(1)}, f32[6400]{0:T(1024)S(1)}, u32[]{:S(2)}, u32[]{:S(2)}) collective-permute-start(f32[6400]{0:T(1024)S(1)} %pad_maximum_fusion.7), channel_id=1, source_target_pairs={{0,32},{8,40},{16,48},{24,56},{32,0},{40,8},{48,16},{56,24},{64,96... | collective-permute-start | bytes 76808 | tf_op jit(solution)/shard_map/ppermute | solution.py:237
  4.6 1.9 %collective-permute-done = f32[6400]{0:T(1024)S(1)} collective-permute-done((f32[6400]{0:T(1024)S(1)}, f32[6400]{0:T(1024)S(1)}, u32[]{:S(2)}, u32[]{:S(2)}) %collective-permute-start) | collective-permute-done | bytes 25632 | tf_op jit(solution)/shard_map/ppermute | solution.py:237
  6.5 4.2 %collective-permute-start.1 = (f32[6400]{0:T(1024)S(1)}, f32[6400]{0:T(1024)S(1)}, u32[]{:S(2)}, u32[]{:S(2)}) collective-permute-start(f32[6400]{0:T(1024)S(1)} %fusion), channel_id=1, source_target_pairs={{0,96},{8,104},{16,112},{24,120},{32,64},{40,72},{48,80},{56,88},{... | collective-permute-start | bytes 76808 | tf_op jit(solution)/shard_map/ppermute | solution.py:237
  12.2 1.8 %collective-permute-start.5 = (bf16[160,1408]{1,0:T(8,128)(2,1)S(1)}, bf16[160,1408]{1,0:T(8,128)(2,1)S(1)}, u32[]{:S(2)}, u32[]{:S(2)}) collective-permute-start(bf16[160,1408]{1,0:T(8,128)(2,1)S(1)} %get-tuple-element.43.refs_6_), channel_id=1, source_target_pairs={{0,24},{8,0},{16,8},{24,16},{32,56},{40,32},{48,40},{56,48},{64,88... | collective-permute-start | bytes 1351688 | tf_op jit(solution)/shard_map/ppermute | solution.py:36
  13.9 3.2 %collective-permute-start.7 = (bf16[160,1408]{1,0:T(8,128)(2,1)S(1)}, bf16[160,1408]{1,0:T(8,128)(2,1)S(1)}, u32[]{:S(2)}, u32[]{:S(2)}) collective-permute-start(bf16[160,1408]{1,0:T(8,128)(2,1)S(1)} %get-tuple-element.44.refs_7_), channel_id=1, source_target_pairs={{0,96},{8,104},{16,112},{24,120},{32,0},{40,8},{48,16},{56,24},{64... | collective-permute-start | bytes 1351688 | tf_op jit(solution)/shard_map/ppermute | solution.py:36
  17.6 5.6 %collective-permute-done.2 = f32[6400]{0:T(1024)S(1)} collective-permute-done((f32[6400]{0:T(1024)S(1)}, f32[6400]{0:T(1024)S(1)}, u32[]{:S(2)}, u32[]{:S(2)}) %collective-permute-start.2) | collective-permute-done | bytes 25632 | tf_op jit(solution)/shard_map/ppermute | solution.py:237
  24.8 3.5 %collective-permute-done.3 = f32[6400]{0:T(1024)S(1)} collective-permute-done((f32[6400]{0:T(1024)S(1)}, f32[6400]{0:T(1024)S(1)}, u32[]{:S(2)}, u32[]{:S(2)}) %collective-permute-start.3) | collective-permute-done | bytes 25632 | tf_op jit(solution)/shard_map/ppermute | solution.py:237
  34.7 2.8 %collective-permute-start.25 = (bf16[160,1408]{1,0:T(8,128)(2,1)S(1)}, bf16[160,1408]{1,0:T(8,128)(2,1)S(1)}, u32[]{:S(2)}, u32[]{:S(2)}) collective-permute-start(bf16[160,1408]{1,0:T(8,128)(2,1)S(1)} %get-tuple-element.44.refs_7_), channel_id=1, source_target_pairs={{0,24},{8,0},{16,8},{24,16},{32,56},{40,32},{48,40},{56,48},{64,88... | collective-permute-start | bytes 1351688 | tf_op jit(solution)/shard_map/ppermute | solution.py:36
  37.5 8.3 %collective-permute-done.24.refs_2_ = bf16[160,1408]{1,0:T(8,128)(2,1)S(1)} collective-permute-done((bf16[160,1408]{1,0:T(8,128)(2,1)S(1)}, bf16[160,1408]{1,0:T(8,128)(2,1)S(1)}, u32[]{:S(2)}, u32[]{:S(2)}) %collective-permute-start.24) | collective-permute-done | bytes 450592 | tf_op jit(solution)/shard_map/ppermute | solution.py:36
  46.2 14.3 %collective-permute-done.25.refs_3_ = bf16[160,1408]{1,0:T(8,128)(2,1)S(1)} collective-permute-done((bf16[160,1408]{1,0:T(8,128)(2,1)S(1)}, bf16[160,1408]{1,0:T(8,128)(2,1)S(1)}, u32[]{:S(2)}, u32[]{:S(2)}) %collective-permute-start.25) | collective-permute-done | bytes 450592 | tf_op jit(solution)/shard_map/ppermute | solution.py:36
  60.5 3.0 %collective-permute-start.34 = (bf16[5120]{0:T(1024)(128)(2,1)S(1)}, bf16[5120]{0:T(1024)(128)(2,1)S(1)}, u32[]{:S(2)}, u32[]{:S(2)}) collective-permute-start(bf16[5120]{0:T(1024)(128)(2,1)S(1)} %max.26), channel_id=1, source_target_pairs={{0,6},{1,7},{2,4},{3,5},{4,2},{5,3},{6,0},{7,1},{8,14},{9,15},{10,... | collective-permute-start | bytes 30728 | tf_op jit(solution)/shard_map/ppermute | solution.py:378
  63.5 1.7 %second_hop.1 = (bf16[80,1280]{1,0:T(8,128)(2,1)S(1)}, bf16[80,1280]{1,0:T(8,128)(2,1)S(1)}, bf16[80,1280]{1,0:T(8,128)(2,1)S(1)}, bf16[80,1280]{1,0:T(8,128)(2,...) custom-call(bf16[128,1280]{1,0:T(8,128)(2,1)S(1)} %pad_maximum_fusio, ...), custom_call_target="tpu_custom_call", output_to_operand_aliasing={{4}: (8, {}), {5}: (9, {}), {6}: (10, {})} | custom-call | tf_op jit(solution)/shard_map/second_hop/pallas_call | solution.py:197
  65.3 3.2 %collective-permute-start.29 = (bf16[80,1280]{1,0:T(8,128)(2,1)S(1)}, bf16[80,1280]{1,0:T(8,128)(2,1)S(1)}, u32[]{:S(2)}, u32[]{:S(2)}) collective-permute-start(bf16[80,1280]{1,0:T(8,128)(2,1)S(1)} %get-tuple-element.53), channel_id=1, source_target_pairs={{0,24},{8,0},{16,8},{24,16},{32,56},{40,32},{48,40},{56,48},{64,88... | collective-permute-start | bytes 614408 | tf_op jit(solution)/shard_map/ppermute | solution.py:36
  70.8 18.6 %collective-permute-done.9.refs_3_ = bf16[400,1280]{1,0:T(8,128)(2,1)S(1)} collective-permute-done((bf16[400,1280]{1,0:T(8,128)(2,1)S(1)}, bf16[400,1280]{1,0:T(8,128)(2,1)S(1)}, u32[]{:S(2)}, u32[]{:S(2)}) %collective-permute-start.9) | collective-permute-done | bytes 1024032 | tf_op jit(solution)/shard_map/ppermute | solution.py:36
  89.5 4.6 %collective-permute-done.8.refs_2_ = bf16[400,1280]{1,0:T(8,128)(2,1)S(1)} collective-permute-done((bf16[400,1280]{1,0:T(8,128)(2,1)S(1)}, bf16[400,1280]{1,0:T(8,128)(2,1)S(1)}, u32[]{:S(2)}, u32[]{:S(2)}) %collective-permute-start.8) | collective-permute-done | bytes 1024032 | tf_op jit(solution)/shard_map/ppermute | solution.py:36
  94.3 2.1 %collective-permute-start.30 = (bf16[80,1280]{1,0:T(8,128)(2,1)S(1)}, bf16[80,1280]{1,0:T(8,128)(2,1)S(1)}, u32[]{:S(2)}, u32[]{:S(2)}) collective-permute-start(bf16[80,1280]{1,0:T(8,128)(2,1)S(1)} %get-tuple-element.54), channel_id=1, source_target_pairs={{0,32},{8,40},{16,48},{24,56},{32,64},{40,72},{48,80},{56,88},{64,... | collective-permute-start | bytes 614408 | tf_op jit(solution)/shard_map/ppermute | solution.py:36
  96.4 3.2 %collective-permute-start.12 = (bf16[160,1280]{1,0:T(8,128)(2,1)S(1)}, bf16[160,1280]{1,0:T(8,128)(2,1)S(1)}, u32[]{:S(2)}, u32[]{:S(2)}) collective-permute-start(bf16[160,1280]{1,0:T(8,128)(2,1)S(1)} %pad_maximum_fusion), channel_id=1, source_target_pairs={{0,24},{8,0},{16,8},{24,16},{32,56},{40,32},{48,40},{56,48},{64,88... | collective-permute-start | bytes 1228808 | tf_op jit(solution)/shard_map/ppermute | solution.py:36
  99.6 3.7 %collective-permute-done.30.refs_2_ = bf16[80,1280]{1,0:T(8,128)(2,1)S(1)} collective-permute-done((bf16[80,1280]{1,0:T(8,128)(2,1)S(1)}, bf16[80,1280]{1,0:T(8,128)(2,1)S(1)}, u32[]{:S(2)}, u32[]{:S(2)}) %collective-permute-start.30) | collective-permute-done | bytes 204832 | tf_op jit(solution)/shard_map/ppermute | solution.py:36
  105.5 1.8 %collective-permute-start.21 = (bf16[160,1280]{1,0:T(8,128)(2,1)S(1)}, bf16[160,1280]{1,0:T(8,128)(2,1)S(1)}, u32[]{:S(2)}, u32[]{:S(2)}) collective-permute-start(bf16[160,1280]{1,0:T(8,128)(2,1)S(1)} %pad_maximum_fusion.3), channel_id=1, source_target_pairs={{0,24},{8,0},{16,8},{24,16},{32,56},{40,32},{48,40},{56,48},{64,88... | collective-permute-start | bytes 1228808 | tf_op jit(solution)/shard_map/ppermute | solution.py:36
  108.4 2.5 %collective-permute-done.31.refs_3_ = bf16[80,1280]{1,0:T(8,128)(2,1)S(1)} collective-permute-done((bf16[80,1280]{1,0:T(8,128)(2,1)S(1)}, bf16[80,1280]{1,0:T(8,128)(2,1)S(1)}, u32[]{:S(2)}, u32[]{:S(2)}) %collective-permute-start.31) | collective-permute-done | bytes 204832 | tf_op jit(solution)/shard_map/ppermute | solution.py:36
  111.2 6.2 %collective-permute-done.23.refs_7_ = bf16[160,1280]{1,0:T(8,128)(2,1)S(1)} collective-permute-done((bf16[160,1280]{1,0:T(8,128)(2,1)S(1)}, bf16[160,1280]{1,0:T(8,128)(2,1)S(1)}, u32[]{:S(2)}, u32[]{:S(2)}) %collective-permute-start.23) | collective-permute-done | bytes 409632 | tf_op jit(solution)/shard_map/ppermute | solution.py:36
  117.4 3.2 %collective-permute-start.13 = (bf16[80,1280]{1,0:T(8,128)(2,1)S(1)}, bf16[80,1280]{1,0:T(8,128)(2,1)S(1)}, u32[]{:S(2)}, u32[]{:S(2)}) collective-permute-start(bf16[80,1280]{1,0:T(8,128)(2,1)S(1)} %slice.88), channel_id=1, source_target_pairs={{0,24},{8,0},{16,8},{24,16},{32,56},{40,32},{48,40},{56,48},{64,88... | collective-permute-start | bytes 614408 | tf_op jit(solution)/shard_map/ppermute | solution.py:36
  122.6 2.0 %shard_map.163 = (bf16[5120,1024]{1,0:T(8,128)(2,1)}, bf16[5120,128]{1,0:T(8,128)(2,1)}, bf16[5120,128]{1,0:T(8,128)(2,1)}) custom-call(bf16[400,1280]{1,0:T(8,128)(2,1)S(1)} %collective-permute-done.14.refs_0_, bf16[400,1280]{1,0:T(8,128)(2,1)S(1)} %collective-permute-done.15.refs_1_, ...), custom_call_target="tpu_custom_call", output_to_operand_aliasing={{0}: (4, {}), {1}: (5, {}), {2}: (6, {})} | custom-call | tf_op jit(solution)/shard_map/pallas_call | solution.py:224
  124.7 1.7 %shard_map.164 = (bf16[5120,1024]{1,0:T(8,128)(2,1)}, bf16[5120,128]{1,0:T(8,128)(2,1)}, bf16[5120,128]{1,0:T(8,128)(2,1)}) custom-call(bf16[160,1280]{1,0:T(8,128)(2,1)S(1)} %collective-permute-done.10.refs_0_, bf16[160,1280]{1,0:T(8,128)(2,1)S(1)} %collective-permute-done.12.refs_1_, ...), custom_call_target="tpu_custom_call", output_to_operand_aliasing={{0}: (8, {}), {1}: (9, {}), {2}: (10, {})} | custom-call | tf_op jit(solution)/shard_map/pallas_call | solution.py:224
  (85 shorter events, 21.2 us)
Async XLA Ops:
  6.5 10.7 %collective-permute-start.1 = (f32[6400]{0:T(1024)S(1)}, f32[6400]{0:T(1024)S(1)}, u32[]{:S(2)}, u32[]{:S(2)}) collective-permute-start(f32[6400]{0:T(1024)S(1)} %fusion), channel_id=1, source_target_pairs={{0,96},{8,104},{16,112},{24,120},{32,64},{40,72},{48,80},{56,88},{... | collective-permute-start | bytes 76808 | tf_op jit(solution)/shard_map/ppermute | solution.py:237
  10.7 17.6 %collective-permute-start.4 = (bf16[160,1408]{1,0:T(8,128)(2,1)S(1)}, bf16[160,1408]{1,0:T(8,128)(2,1)S(1)}, u32[]{:S(2)}, u32[]{:S(2)}) collective-permute-start(bf16[160,1408]{1,0:T(8,128)(2,1)S(1)} %get-tuple-element.43.refs_6_), channel_id=1, source_target_pairs={{0,8},{8,16},{16,24},{24,0},{32,40},{40,48},{48,56},{56,32},{64,72... | collective-permute-start | bytes 1351688 | tf_op jit(solution)/shard_map/ppermute | solution.py:36
  12.2 16.1 %collective-permute-start.5 = (bf16[160,1408]{1,0:T(8,128)(2,1)S(1)}, bf16[160,1408]{1,0:T(8,128)(2,1)S(1)}, u32[]{:S(2)}, u32[]{:S(2)}) collective-permute-start(bf16[160,1408]{1,0:T(8,128)(2,1)S(1)} %get-tuple-element.43.refs_6_), channel_id=1, source_target_pairs={{0,24},{8,0},{16,8},{24,16},{32,56},{40,32},{48,40},{56,48},{64,88... | collective-permute-start | bytes 1351688 | tf_op jit(solution)/shard_map/ppermute | solution.py:36
  13.9 14.4 %collective-permute-start.6 = (bf16[160,1408]{1,0:T(8,128)(2,1)S(1)}, bf16[160,1408]{1,0:T(8,128)(2,1)S(1)}, u32[]{:S(2)}, u32[]{:S(2)}) collective-permute-start(bf16[160,1408]{1,0:T(8,128)(2,1)S(1)} %get-tuple-element.44.refs_7_), channel_id=1, source_target_pairs={{0,32},{8,40},{16,48},{24,56},{32,64},{40,72},{48,80},{56,88},{64,... | collective-permute-start | bytes 1351688 | tf_op jit(solution)/shard_map/ppermute | solution.py:36
  13.9 14.4 %collective-permute-start.7 = (bf16[160,1408]{1,0:T(8,128)(2,1)S(1)}, bf16[160,1408]{1,0:T(8,128)(2,1)S(1)}, u32[]{:S(2)}, u32[]{:S(2)}) collective-permute-start(bf16[160,1408]{1,0:T(8,128)(2,1)S(1)} %get-tuple-element.44.refs_7_), channel_id=1, source_target_pairs={{0,96},{8,104},{16,112},{24,120},{32,0},{40,8},{48,16},{56,24},{64... | collective-permute-start | bytes 1351688 | tf_op jit(solution)/shard_map/ppermute | solution.py:36
  29.8 38.7 %collective-permute-start.15 = (bf16[400,1280]{1,0:T(8,128)(2,1)S(1)}, bf16[400,1280]{1,0:T(8,128)(2,1)S(1)}, u32[]{:S(2)}, u32[]{:S(2)}) collective-permute-start(bf16[400,1280]{1,0:T(8,128)(2,1)S(1)} %get-tuple-element.48), channel_id=1, source_target_pairs={{0,24},{8,0},{16,8},{24,16},{32,56},{40,32},{48,40},{56,48},{64,88... | collective-permute-start | bytes 3072008 | tf_op jit(solution)/shard_map/ppermute | solution.py:36
  31.4 14.4 %collective-permute-start.24 = (bf16[160,1408]{1,0:T(8,128)(2,1)S(1)}, bf16[160,1408]{1,0:T(8,128)(2,1)S(1)}, u32[]{:S(2)}, u32[]{:S(2)}) collective-permute-start(bf16[160,1408]{1,0:T(8,128)(2,1)S(1)} %get-tuple-element.44.refs_7_), channel_id=1, source_target_pairs={{0,8},{8,16},{16,24},{24,0},{32,40},{40,48},{48,56},{56,32},{64,72... | collective-permute-start | bytes 1351688 | tf_op jit(solution)/shard_map/ppermute | solution.py:36
  31.9 37.3 %collective-permute-start.14 = (bf16[400,1280]{1,0:T(8,128)(2,1)S(1)}, bf16[400,1280]{1,0:T(8,128)(2,1)S(1)}, u32[]{:S(2)}, u32[]{:S(2)}) collective-permute-start(bf16[400,1280]{1,0:T(8,128)(2,1)S(1)} %get-tuple-element.47), channel_id=1, source_target_pairs={{0,8},{8,16},{16,24},{24,0},{32,40},{40,48},{48,56},{56,32},{64,72... | collective-permute-start | bytes 3072008 | tf_op jit(solution)/shard_map/ppermute | solution.py:36
  34.7 25.7 %collective-permute-start.25 = (bf16[160,1408]{1,0:T(8,128)(2,1)S(1)}, bf16[160,1408]{1,0:T(8,128)(2,1)S(1)}, u32[]{:S(2)}, u32[]{:S(2)}) collective-permute-start(bf16[160,1408]{1,0:T(8,128)(2,1)S(1)} %get-tuple-element.44.refs_7_), channel_id=1, source_target_pairs={{0,24},{8,0},{16,8},{24,16},{32,56},{40,32},{48,40},{56,48},{64,88... | collective-permute-start | bytes 1351688 | tf_op jit(solution)/shard_map/ppermute | solution.py:36
  37.5 26.0 %collective-permute-start.26 = (bf16[160,1408]{1,0:T(8,128)(2,1)S(1)}, bf16[160,1408]{1,0:T(8,128)(2,1)S(1)}, u32[]{:S(2)}, u32[]{:S(2)}) collective-permute-start(bf16[160,1408]{1,0:T(8,128)(2,1)S(1)} %get-tuple-element.43.refs_6_), channel_id=1, source_target_pairs={{0,32},{8,40},{16,48},{24,56},{32,64},{40,72},{48,80},{56,88},{64,... | collective-permute-start | bytes 1351688 | tf_op jit(solution)/shard_map/ppermute | solution.py:36
  45.8 17.7 %collective-permute-start.27 = (bf16[160,1408]{1,0:T(8,128)(2,1)S(1)}, bf16[160,1408]{1,0:T(8,128)(2,1)S(1)}, u32[]{:S(2)}, u32[]{:S(2)}) collective-permute-start(bf16[160,1408]{1,0:T(8,128)(2,1)S(1)} %get-tuple-element.43.refs_6_), channel_id=1, source_target_pairs={{0,96},{8,104},{16,112},{24,120},{32,0},{40,8},{48,16},{56,24},{64... | collective-permute-start | bytes 1351688 | tf_op jit(solution)/shard_map/ppermute | solution.py:36
  60.5 33.7 %collective-permute-start.34 = (bf16[5120]{0:T(1024)(128)(2,1)S(1)}, bf16[5120]{0:T(1024)(128)(2,1)S(1)}, u32[]{:S(2)}, u32[]{:S(2)}) collective-permute-start(bf16[5120]{0:T(1024)(128)(2,1)S(1)} %max.26), channel_id=1, source_target_pairs={{0,6},{1,7},{2,4},{3,5},{4,2},{5,3},{6,0},{7,1},{8,14},{9,15},{10,... | collective-permute-start | bytes 30728 | tf_op jit(solution)/shard_map/ppermute | solution.py:378
  65.2 29.1 %collective-permute-start.28 = (bf16[80,1280]{1,0:T(8,128)(2,1)S(1)}, bf16[80,1280]{1,0:T(8,128)(2,1)S(1)}, u32[]{:S(2)}, u32[]{:S(2)}) collective-permute-start(bf16[80,1280]{1,0:T(8,128)(2,1)S(1)} %get-tuple-element.52), channel_id=1, source_target_pairs={{0,8},{8,16},{16,24},{24,0},{32,40},{40,48},{48,56},{56,32},{64,72... | collective-permute-start | bytes 614408 | tf_op jit(solution)/shard_map/ppermute | solution.py:36
  65.3 31.1 %collective-permute-start.29 = (bf16[80,1280]{1,0:T(8,128)(2,1)S(1)}, bf16[80,1280]{1,0:T(8,128)(2,1)S(1)}, u32[]{:S(2)}, u32[]{:S(2)}) collective-permute-start(bf16[80,1280]{1,0:T(8,128)(2,1)S(1)} %get-tuple-element.53), channel_id=1, source_target_pairs={{0,24},{8,0},{16,8},{24,16},{32,56},{40,32},{48,40},{56,48},{64,88... | collective-permute-start | bytes 614408 | tf_op jit(solution)/shard_map/ppermute | solution.py:36
  68.5 20.8 %collective-permute-start.9 = (bf16[400,1280]{1,0:T(8,128)(2,1)S(1)}, bf16[400,1280]{1,0:T(8,128)(2,1)S(1)}, u32[]{:S(2)}, u32[]{:S(2)}) collective-permute-start(bf16[400,1280]{1,0:T(8,128)(2,1)S(1)} %get-tuple-element.46), channel_id=1, source_target_pairs={{0,96},{8,104},{16,112},{24,120},{32,0},{40,8},{48,16},{56,24},{64... | collective-permute-start | bytes 3072008 | tf_op jit(solution)/shard_map/ppermute | solution.py:36
  69.2 24.8 %collective-permute-start.8 = (bf16[400,1280]{1,0:T(8,128)(2,1)S(1)}, bf16[400,1280]{1,0:T(8,128)(2,1)S(1)}, u32[]{:S(2)}, u32[]{:S(2)}) collective-permute-start(bf16[400,1280]{1,0:T(8,128)(2,1)S(1)} %get-tuple-element.45), channel_id=1, source_target_pairs={{0,32},{8,40},{16,48},{24,56},{32,64},{40,72},{48,80},{56,88},{64,... | collective-permute-start | bytes 3072008 | tf_op jit(solution)/shard_map/ppermute | solution.py:36
  89.4 14.0 %collective-permute-start.16 = (bf16[160,1280]{1,0:T(8,128)(2,1)S(1)}, bf16[160,1280]{1,0:T(8,128)(2,1)S(1)}, u32[]{:S(2)}, u32[]{:S(2)}) collective-permute-start(bf16[160,1280]{1,0:T(8,128)(2,1)S(1)} %pad_maximum_fusion.1), channel_id=1, source_target_pairs={{0,32},{8,40},{16,48},{24,56},{32,64},{40,72},{48,80},{56,88},{64,... | collective-permute-start | bytes 1228808 | tf_op jit(solution)/shard_map/ppermute | solution.py:36
  94.2 11.3 %collective-permute-start.10 = (bf16[160,1280]{1,0:T(8,128)(2,1)S(1)}, bf16[160,1280]{1,0:T(8,128)(2,1)S(1)}, u32[]{:S(2)}, u32[]{:S(2)}) collective-permute-start(bf16[160,1280]{1,0:T(8,128)(2,1)S(1)} %pad_maximum_fusion), channel_id=1, source_target_pairs={{0,8},{8,16},{16,24},{24,0},{32,40},{40,48},{48,56},{56,32},{64,72... | collective-permute-start | bytes 1228808 | tf_op jit(solution)/shard_map/ppermute | solution.py:36
  96.4 11.1 %collective-permute-start.12 = (bf16[160,1280]{1,0:T(8,128)(2,1)S(1)}, bf16[160,1280]{1,0:T(8,128)(2,1)S(1)}, u32[]{:S(2)}, u32[]{:S(2)}) collective-permute-start(bf16[160,1280]{1,0:T(8,128)(2,1)S(1)} %pad_maximum_fusion), channel_id=1, source_target_pairs={{0,24},{8,0},{16,8},{24,16},{32,56},{40,32},{48,40},{56,48},{64,88... | collective-permute-start | bytes 1228808 | tf_op jit(solution)/shard_map/ppermute | solution.py:36
  103.4 14.0 %collective-permute-start.23 = (bf16[160,1280]{1,0:T(8,128)(2,1)S(1)}, bf16[160,1280]{1,0:T(8,128)(2,1)S(1)}, u32[]{:S(2)}, u32[]{:S(2)}) collective-permute-start(bf16[160,1280]{1,0:T(8,128)(2,1)S(1)} %pad_maximum_fusion.5), channel_id=1, source_target_pairs={{0,96},{8,104},{16,112},{24,120},{32,0},{40,8},{48,16},{56,24},{64... | collective-permute-start | bytes 1228808 | tf_op jit(solution)/shard_map/ppermute | solution.py:36
  104.1 13.2 %collective-permute-start.22 = (bf16[160,1280]{1,0:T(8,128)(2,1)S(1)}, bf16[160,1280]{1,0:T(8,128)(2,1)S(1)}, u32[]{:S(2)}, u32[]{:S(2)}) collective-permute-start(bf16[160,1280]{1,0:T(8,128)(2,1)S(1)} %pad_maximum_fusion.4), channel_id=1, source_target_pairs={{0,32},{8,40},{16,48},{24,56},{32,64},{40,72},{48,80},{56,88},{64,... | collective-permute-start | bytes 1228808 | tf_op jit(solution)/shard_map/ppermute | solution.py:36
  105.5 11.9 %collective-permute-start.21 = (bf16[160,1280]{1,0:T(8,128)(2,1)S(1)}, bf16[160,1280]{1,0:T(8,128)(2,1)S(1)}, u32[]{:S(2)}, u32[]{:S(2)}) collective-permute-start(bf16[160,1280]{1,0:T(8,128)(2,1)S(1)} %pad_maximum_fusion.3), channel_id=1, source_target_pairs={{0,24},{8,0},{16,8},{24,16},{32,56},{40,32},{48,40},{56,48},{64,88... | collective-permute-start | bytes 1228808 | tf_op jit(solution)/shard_map/ppermute | solution.py:36
  107.5 17.2 %collective-permute-start.20 = (bf16[160,1280]{1,0:T(8,128)(2,1)S(1)}, bf16[160,1280]{1,0:T(8,128)(2,1)S(1)}, u32[]{:S(2)}, u32[]{:S(2)}) collective-permute-start(bf16[160,1280]{1,0:T(8,128)(2,1)S(1)} %pad_maximum_fusion.2), channel_id=1, source_target_pairs={{0,8},{8,16},{16,24},{24,0},{32,40},{40,48},{48,56},{56,32},{64,72... | collective-permute-start | bytes 1228808 | tf_op jit(solution)/shard_map/ppermute | solution.py:36
  110.9 15.5 %collective-permute-start.17 = (bf16[80,1280]{1,0:T(8,128)(2,1)S(1)}, bf16[80,1280]{1,0:T(8,128)(2,1)S(1)}, u32[]{:S(2)}, u32[]{:S(2)}) collective-permute-start(bf16[80,1280]{1,0:T(8,128)(2,1)S(1)} %slice.91), channel_id=1, source_target_pairs={{0,32},{8,40},{16,48},{24,56},{32,64},{40,72},{48,80},{56,88},{64,... | collective-permute-start | bytes 614408 | tf_op jit(solution)/shard_map/ppermute | solution.py:36
  (11 other events, 74.4 us)
